TPU v7x, 32 devices: a whole 2x2x4 slice. The times are simulated.
32 devices in a mesh: dp: 4 (over x, core), table: 8 (over z, y).
Axes of the slice: x: 2, y: 2, z: 4, core: 2. Of those that a mesh axis runs over, the one named last changes fastest.
Arguments:
- out_grad: bfloat16 [32768, 1024], P(('dp', 'table')), may hold values from -0.1875 to 0.1875
- pair_cells: int32 [32768, 8, 32], P(('dp', 'table')), may hold values from 0 to 4095
- weight_codes: int32 [32768, 8, 32], P(('dp', 'table')), may hold values from -127 to 127
- head_scale: float32 [8], replicated, may hold values from 0.5 to 2
- touch_slots: int32 [8, 8, 4], replicated, may hold values from 0 to 7
Outputs:
- grad_rows: bfloat16 [8192, 1024], P('table', 'dp')
All inputs are finite; a program needn't handle non-finite values.
Results may differ from a plain program's by a relative error of at most 0.0098.
Values may be sent and summed in bfloat16 or wider, within the bound.
No kernel may reach another device: no remote copies, remote signals or barrier semaphores. Data moves between devices by JAX's collectives and lax.ppermute only.
A program may use at most 128 MiB of HBM per device.

v0:
```python
import functools

import jax
import jax.numpy as jnp
from jax import lax
from jax.experimental import pallas as pl
from jax.experimental.pallas import tpu as pltpu
from jax.sharding import PartitionSpec as P


ROWS = 128
TOUCH = 32
OWN = 8
CELL_BITS = 12
CODE_BIAS = 128
BLOCK = 128
SIDE = 64
CHUNKS = 8
EARLY = 3


def fill_coef(scale_ref, cells_ref, codes_ref, write, low_ref, high_ref, weight_ref, table_ref):
    pairs, block = cells_ref.shape
    heads = scale_ref.shape[0]
    packed = (cells_ref[...] | ((codes_ref[...] + CODE_BIAS) << CELL_BITS)).T
    stride = table_ref.shape[0] // TOUCH
    tile = (packed >> 7) & (TOUCH - 1)
    upper = (packed >> 6) & 1
    low_ref[...] = (packed & (SIDE - 1)).astype(jnp.float32)
    high_ref[...] = (tile + TOUCH * upper).astype(jnp.float32)
    head = lax.broadcasted_iota(jnp.int32, (1, pairs), 1) // (pairs // heads)
    scale = jnp.zeros((1, pairs), jnp.float32)
    for h in range(heads):
        scale = jnp.where(head == h, scale_ref[h] / 128.0, scale)
    weight_ref[...] = ((packed >> CELL_BITS) - CODE_BIAS).astype(jnp.float32) * scale
    iota = lax.broadcasted_iota(jnp.int32, (SIDE, pairs), 0).astype(jnp.float32).astype(jnp.bfloat16)

    def spread(ref, token):
        row = jnp.broadcast_to(ref[pl.ds(token, 1), :], (16, pairs)).astype(jnp.bfloat16)
        return jnp.concatenate([row] * (SIDE // 16), axis=0)

    for token in range(block):
        low_hot = jnp.where(spread(low_ref, token) == iota, jnp.bfloat16(1), jnp.bfloat16(0))
        high_hot = jnp.where(spread(high_ref, token) == iota, spread(weight_ref, token), jnp.bfloat16(0))
        table = lax.dot_general(
            high_hot, low_hot, (((1,), (1,)), ((), ())), preferred_element_type=jnp.float32
        )
        table = jnp.concatenate([table[:TOUCH], table[TOUCH:]], axis=1)
        table_ref[pl.ds(token, TOUCH, stride=stride), :] = table
    for j in range(TOUCH):
        write(j, table_ref[pl.ds(j * stride, block), :].astype(jnp.bfloat16))


def distance_at(position, groups):
    half = groups // 2
    if isinstance(position, int):
        return half + position if position < half else groups - 1 - position
    return jnp.where(position < half, half + position, groups - 1 - position)


def put_products(flip, coef, out_refs):
    product = jnp.dot(flip, coef, preferred_element_type=jnp.float32)
    for n, out_ref in enumerate(out_refs):
        width = out_ref.shape[2]
        for c in range(out_ref.shape[1]):
            part = product[n * width : (n + 1) * width, c * ROWS : (c + 1) * ROWS]
            out_ref[0, c] = part.astype(jnp.bfloat16)


def first_kernel(place_ref, scale_ref, cells_ref, codes_ref, *refs, groups):
    replicas = (len(refs) - 9) // 2
    grad_refs, (coef_hbm, flip_hbm), out_refs = refs[:replicas], refs[replicas : replicas + 2], refs[replicas + 2 : -7]
    low_ref, high_ref, weight_ref, table_ref, coef_ref, flip_ref, semaphores = refs[-7:]
    step = pl.program_id(0)
    block = cells_ref.shape[1]
    width = grad_refs[0].shape[1]
    blocks = coef_ref.shape[0] // block
    span = coef_ref.shape[1] // groups

    saves = [
        pltpu.make_async_copy(coef_ref, coef_hbm, semaphores.at[0]),
        pltpu.make_async_copy(flip_ref, flip_hbm, semaphores.at[1]),
    ]

    @pl.when(step < blocks)
    def _():
        rows = pl.ds(pl.multiple_of(step * block, block), block)

        def write(j, part):
            coef_ref[rows, j * ROWS : (j + 1) * ROWS] = part

        for n in range(replicas):
            flip_ref[n * width : (n + 1) * width, rows] = grad_refs[n][...].T
        fill_coef(scale_ref, cells_ref, codes_ref, write, low_ref, high_ref, weight_ref, table_ref)

    @pl.when(step >= blocks)
    def _():
        @pl.when(step == blocks)
        def _():
            for copy in saves:
                copy.start()

        owner = place_ref[1] ^ distance_at(step - blocks, groups)
        coef = coef_ref[:, pl.ds(pl.multiple_of(owner * span, span), span)]
        put_products(flip_ref[...], coef, out_refs)

    @pl.when(step == pl.num_programs(0) - 1)
    def _():
        for copy in saves:
            copy.wait()


def first_products(place, head_scale, cells, codes, grads, replicas, width, capacity, groups, length):
    pairs, tokens = cells.shape
    blocks = tokens // BLOCK
    last = blocks - 1
    spec = pl.BlockSpec((pairs, BLOCK), lambda i, *_: (0, jnp.minimum(i, last)))
    outs = [jax.ShapeDtypeStruct((length, capacity, width, ROWS), jnp.bfloat16) for _ in range(replicas)]
    cells_all = TOUCH * ROWS
    return pl.pallas_call(
        functools.partial(first_kernel, groups=groups),
        grid_spec=pltpu.PrefetchScalarGridSpec(
            num_scalar_prefetch=2,
            grid=(blocks + length,),
            in_specs=[spec, spec]
            + [
                pl.BlockSpec((BLOCK, width), lambda i, place, scale, m=m: (jnp.minimum(i, last), place[0] ^ m))
                for m in range(replicas)
            ],
            out_specs=[pl.BlockSpec(memory_space=pl.ANY), pl.BlockSpec(memory_space=pl.ANY)]
            + [
                pl.BlockSpec((1, capacity, width, ROWS), lambda i, *_: (jnp.maximum(i - blocks, 0), 0, 0, 0))
                for _ in outs
            ],
            scratch_shapes=[
                pltpu.VMEM((BLOCK, pairs), jnp.float32),
                pltpu.VMEM((BLOCK, pairs), jnp.float32),
                pltpu.VMEM((BLOCK, pairs), jnp.float32),
                pltpu.VMEM((TOUCH * (BLOCK + 8), ROWS), jnp.float32),
                pltpu.VMEM((tokens, cells_all), jnp.bfloat16),
                pltpu.VMEM((replicas * width, tokens), jnp.bfloat16),
                pltpu.SemaphoreType.DMA((2,)),
            ],
        ),
        out_shape=[
            jax.ShapeDtypeStruct((tokens, cells_all), jnp.bfloat16),
            jax.ShapeDtypeStruct((replicas * width, tokens), jnp.bfloat16),
        ]
        + outs,
        cost_estimate=pl.CostEstimate(
            flops=2 * tokens * pairs * cells_all * 4, transcendentals=0, bytes_accessed=tokens * cells_all * 4
        ),
        compiler_params=pltpu.CompilerParams(vmem_limit_bytes=30 << 20),
        name="first_products",
    )(place, head_scale, *[pltpu.with_memory_space_constraint(a, pltpu.HBM) for a in [cells, codes] + [grads] * replicas])


def rest_kernel(place_ref, coef_ref, flip_ref, after_ref, *out_refs):
    put_products(flip_ref[...], coef_ref[...], out_refs)


def rest_products(place, coef, flip, after, replicas, width, capacity, groups, first):
    tokens = coef.shape[0]
    length = groups - first
    return pl.pallas_call(
        rest_kernel,
        grid_spec=pltpu.PrefetchScalarGridSpec(
            num_scalar_prefetch=1,
            grid=(length,),
            in_specs=[
                pl.BlockSpec((tokens, capacity * ROWS), lambda i, place: (0, place[1] ^ distance_at(first + i, groups))),
                pl.BlockSpec(flip.shape, lambda i, place: (0, 0)),
                pl.BlockSpec(memory_space=pl.ANY),
            ],
            out_specs=[
                pl.BlockSpec((1, capacity, width, ROWS), lambda i, place: (i, 0, 0, 0)) for _ in range(replicas)
            ],
        ),
        out_shape=[
            jax.ShapeDtypeStruct((length, capacity, width, ROWS), jnp.bfloat16) for _ in range(replicas)
        ],
        cost_estimate=pl.CostEstimate(
            flops=2 * tokens * length * capacity * ROWS * width * replicas,
            transcendentals=0,
            bytes_accessed=2 * length * capacity * ROWS * (tokens + replicas * width) + 2 * replicas * width * tokens,
        ),
        compiler_params=pltpu.CompilerParams(vmem_limit_bytes=24 << 20),
        name="rest_products",
    )(place, coef, flip, after)


def add_kernel(*refs, plan):
    count = len(refs) - len(plan)
    for out_ref, terms in zip(refs[count:], plan):
        size = out_ref.shape[0]
        total = 0.0
        for n, at in terms:
            total = total + refs[n][at * size : (at + 1) * size].astype(jnp.float32)
        out_ref[...] = total.astype(jnp.bfloat16)


def add_blocks(sums, size):
    arrays = []
    plan = []
    for terms in sums:
        row = []
        for array, at in terms:
            known = [n for n, other in enumerate(arrays) if other is array]
            if not known:
                known = [len(arrays)]
                arrays.append(array)
            row.append((known[0], at))
        plan.append(tuple(row))
    shape = (size,) + arrays[0].shape[1:]
    spec = pl.BlockSpec(memory_space=pltpu.VMEM)
    return pl.pallas_call(
        functools.partial(add_kernel, plan=tuple(plan)),
        in_specs=[spec for _ in arrays],
        out_specs=[spec for _ in plan],
        out_shape=[pltpu.VMEM(shape, jnp.bfloat16) for _ in plan],
        compiler_params=pltpu.CompilerParams(vmem_limit_bytes=4 << 20),
        name="add_blocks",
    )(*[pltpu.with_memory_space_constraint(array, pltpu.VMEM) for array in arrays])


def gather_kernel(place_ref, slot_ref, *refs):
    part_refs, out_ref, sum_ref = refs[:-2], refs[-2], refs[-1]
    groups = len(part_refs)
    capacity = part_refs[0].shape[1]
    owner = place_ref[1]
    sum_ref[...] = jnp.zeros(sum_ref.shape, jnp.float32)
    for n, part_ref in enumerate(part_refs):
        for c in range(capacity):
            slot = slot_ref[((owner ^ n) * groups + owner) * capacity + c]
            sum_ref[slot] += part_ref[0, c].astype(jnp.float32)
    for k in range(OWN):
        out_ref[pl.ds(k * ROWS, ROWS), :] = sum_ref[k].T.astype(jnp.bfloat16)


def gather_tiles(place, slots, parts):
    width = parts[0].shape[2]
    scalars = pl.BlockSpec(memory_space=pltpu.SMEM)
    spec = pl.BlockSpec(memory_space=pltpu.VMEM)
    return pl.pallas_call(
        gather_kernel,
        in_specs=[scalars, scalars] + [spec for _ in parts],
        out_specs=spec,
        scratch_shapes=[pltpu.VMEM((OWN, width, ROWS), jnp.float32)],
        out_shape=jax.ShapeDtypeStruct((OWN * ROWS, width), jnp.bfloat16),
        compiler_params=pltpu.CompilerParams(vmem_limit_bytes=6 << 20),
        name="gather_tiles",
    )(place, slots, *[pltpu.with_memory_space_constraint(part, pltpu.VMEM) for part in parts])


def body(out_grad, pair_cells, weight_codes, head_scale, touch_slots, *, replicas):
    tokens, value = out_grad.shape
    width = value // replicas
    groups = touch_slots.shape[0]
    capacity = touch_slots.shape[2]
    pairs = pair_cells.shape[1] * pair_cells.shape[2]
    place = jnp.stack([lax.axis_index("dp"), lax.axis_index("table")]).astype(jnp.int32)
    by_pair = lambda array: array.transpose(1, 2, 0).reshape(pairs, tokens)

    def swap(array, axis, bit):
        return lax.ppermute(array, axis, [(i, i ^ bit) for i in range(lax.axis_size(axis))])

    chunks = min(CHUNKS, groups)
    size = groups // chunks
    early = max(1, EARLY * chunks // CHUNKS) * size
    pieces = [{m: [] for m in range(0, replicas, 2)} for _ in range(chunks)]

    def take(outs, first):
        order = sorted(range(replicas), reverse=True)
        for m in order:
            array = swap(outs[m], "dp", 1) if m & 1 else outs[m]
            for n in range(array.shape[0] // size):
                pieces[first // size + n][m & ~1].append((array, n))

    def send_far(first, stop):
        some = pieces[first:stop]
        bit = 2
        sent = None
        while bit < replicas:
            masks = [m for m in sorted(some[0], reverse=True) if m & bit]
            sums = iter(add_blocks([piece.pop(m) for piece in some for m in masks], size))
            for piece in some:
                for m in masks:
                    total = next(sums)
                    sent = total if sent is None else sent
                    piece[m ^ bit].append((swap(total, "dp", bit), 0))
            bit *= 2
        return sent

    coef, flip, *outs = first_products(
        place, head_scale, by_pair(pair_cells), by_pair(weight_codes), out_grad, replicas, width, capacity, groups, early
    )
    take(outs, 0)
    sent = send_far(0, early // size)
    outs = rest_products(place, coef, flip, outs[0] if sent is None else sent, replicas, width, capacity, groups, early)
    take(outs, early)
    send_far(early // size, chunks)
    parts = {}
    for chunk, piece in enumerate(pieces):
        (mine,) = add_blocks([piece[0]], size)
        for i in range(size):
            distance = distance_at(chunk * size + i, groups)
            part = mine if size == 1 else mine[i : i + 1]
            parts[distance] = swap(part, "table", distance) if distance else part
    return gather_tiles(place, touch_slots.reshape(-1), [parts[n] for n in range(groups)])


def solution(mesh):
    return jax.shard_map(
        functools.partial(body, replicas=mesh.shape["dp"]),
        mesh=mesh,
        in_specs=(
            P(("dp", "table"), None),
            P(("dp", "table"), None, None),
            P(("dp", "table"), None, None),
            P(),
            P(),
        ),
        out_specs=P("table", "dp"),
        check_vma=False,
    )
```

profile of v0, /device:TPU:0, one launch (start us, length us, event | category | flops | bytes accessed | tf_op | source)
XLA Modules:
  0.0 106.4 jit_solution(14082273433552173149)
XLA Ops:
  0.1 0.7 copy-done.4
  0.7 19.2 %first_products.1 = (bf16[1024,4096]{1,0:T(8,128)(2,1)S(1)}, bf16[1024,1024]{1,0:T(8,128)(2,1)S(1)}, bf16[3,4,256,128]{3,2,1,0:T(8,128)(2,1)S(1)}, bf16[3,4,256,...) custom-call(s32[2]{0:T(128)S(1)} %pad_add_fusion.place_ref, ...), custom_call_target="tpu_custom_call" | custom-call | flops 8589934592 | bytes 16777216 | tf_op jit(solution)/shard_map/first_products/pallas_call | solution.py:120
  19.9 0.5 collective-permute-start
  20.4 1.9 %collective-permute-done.refs_0_ = bf16[3,4,256,128]{3,2,1,0:T(8,128)(2,1)S(1)} collective-permute-done((bf16[3,4,256,128]{3,2,1,0:T(8,128)(2,1)S(1)}, bf16[3,4,256,128]{3,2,1,0:T(8,128)(2,1)S(1)}, u32[]{:S(2)}, u32[]{:S(2)}) %collective-permute-start) | collective-permute-done | bytes 786464 | tf_op jit(solution)/shard_map/ppermute | solution.py:265
  22.4 0.2 add_blocks.10
  22.5 7.3 %rest_products.1 = (bf16[5,4,256,128]{3,2,1,0:T(8,128)(2,1)S(1)}, bf16[5,4,256,128]{3,2,1,0:T(8,128)(2,1)S(1)}, bf16[5,4,256,128]{3,2,1,0:T(8,128)(2,1)S(1)}, bf16[5,4,256,128]{3,2,1,0:T(8,128)(2,1)S(1)}) custom-call(s32[2]{0:T(128)S(1)} %pad_add_fusion.place_ref, bf16[1024,4096]{1,0:T(8,128)(2,1)S(1)} %get-tuple-element.23.coef_ref, ...), custom_call_target="tpu_custom_call" | custom-call | flops 5368709120 | bytes 12582912 | tf_op jit(solution)/shard_map/rest_products/pallas_call | solution.py:165
  29.9 0.4 collective-permute-start.2
  30.3 0.2 collective-permute-start.1
  30.4 0.3 collective-permute-start.10
  30.8 2.6 %collective-permute-start.11 = (bf16[1,4,256,128]{3,2,1,0:T(8,128)(2,1)S(1)}, bf16[1,4,256,128]{3,2,1,0:T(8,128)(2,1)S(1)}, u32[]{:S(2)}, u32[]{:S(2)}) collective-permute-start(bf16[1,4,256,128]{3,2,1,0:T(8,128)(2,1)S(1)} %get-tuple-element.27.after_ref), channel_id=1, source_target_pairs={{0,16},{8,24},{16,0},{24,8},{1,17},{9,25},{17,1},{25,9},{2,18},{10... | collective-permute-start | bytes 786440 | tf_op jit(solution)/shard_map/ppermute | solution.py:265
  33.4 2.4 %collective-permute-start.13 = (bf16[1,4,256,128]{3,2,1,0:T(8,128)(2,1)S(1)}, bf16[1,4,256,128]{3,2,1,0:T(8,128)(2,1)S(1)}, u32[]{:S(2)}, u32[]{:S(2)}) collective-permute-start(bf16[1,4,256,128]{3,2,1,0:T(8,128)(2,1)S(1)} %get-tuple-element.38), channel_id=1, source_target_pairs={{0,16},{8,24},{16,0},{24,8},{1,17},{9,25},{17,1},{25,9},{2,18},{10... | collective-permute-start | bytes 786440 | tf_op jit(solution)/shard_map/ppermute | solution.py:265
  35.8 0.3 add_blocks.11
  36.1 2.6 %collective-permute-start.17 = (bf16[1,4,256,128]{3,2,1,0:T(8,128)(2,1)S(1)}, bf16[1,4,256,128]{3,2,1,0:T(8,128)(2,1)S(1)}, u32[]{:S(2)}, u32[]{:S(2)}) collective-permute-start(bf16[1,4,256,128]{3,2,1,0:T(8,128)(2,1)S(1)} %get-tuple-element.40), channel_id=1, source_target_pairs={{0,16},{8,24},{16,0},{24,8},{1,17},{9,25},{17,1},{25,9},{2,18},{10... | collective-permute-start | bytes 786440 | tf_op jit(solution)/shard_map/ppermute | solution.py:265
  38.8 1.8 %collective-permute-done.11.refs_2_ = bf16[1,4,256,128]{3,2,1,0:T(8,128)(2,1)S(1)} collective-permute-done((bf16[1,4,256,128]{3,2,1,0:T(8,128)(2,1)S(1)}, bf16[1,4,256,128]{3,2,1,0:T(8,128)(2,1)S(1)}, u32[]{:S(2)}, u32[]{:S(2)}) %collective-permute-start.11) | collective-permute-done | bytes 262176 | tf_op jit(solution)/shard_map/ppermute | solution.py:265
  40.6 2.0 %collective-permute-start.8 = (bf16[1,4,256,128]{3,2,1,0:T(8,128)(2,1)S(1)}, bf16[1,4,256,128]{3,2,1,0:T(8,128)(2,1)S(1)}, u32[]{:S(2)}, u32[]{:S(2)}) collective-permute-start(bf16[1,4,256,128]{3,2,1,0:T(8,128)(2,1)S(1)} %get-tuple-element.35), channel_id=1, source_target_pairs={{0,16},{8,24},{16,0},{24,8},{1,17},{9,25},{17,1},{25,9},{2,18},{10... | collective-permute-start | bytes 786440 | tf_op jit(solution)/shard_map/ppermute | solution.py:265
  42.6 0.1 add_blocks.16
  42.7 3.5 %collective-permute-done.15.refs_2_ = bf16[1,4,256,128]{3,2,1,0:T(8,128)(2,1)S(1)} collective-permute-done((bf16[1,4,256,128]{3,2,1,0:T(8,128)(2,1)S(1)}, bf16[1,4,256,128]{3,2,1,0:T(8,128)(2,1)S(1)}, u32[]{:S(2)}, u32[]{:S(2)}) %collective-permute-start.15) | collective-permute-done | bytes 262176 | tf_op jit(solution)/shard_map/ppermute | solution.py:265
  46.2 0.1 add_blocks.18
  46.3 2.1 %collective-permute-start.6 = (bf16[1,4,256,128]{3,2,1,0:T(8,128)(2,1)S(1)}, bf16[1,4,256,128]{3,2,1,0:T(8,128)(2,1)S(1)}, u32[]{:S(2)}, u32[]{:S(2)}) collective-permute-start(bf16[1,4,256,128]{3,2,1,0:T(8,128)(2,1)S(1)} %get-tuple-element.34), channel_id=1, source_target_pairs={{0,16},{8,24},{16,0},{24,8},{1,17},{9,25},{17,1},{25,9},{2,18},{10... | collective-permute-start | bytes 786440 | tf_op jit(solution)/shard_map/ppermute | solution.py:265
  48.4 3.4 %collective-permute-done.13.refs_2_ = bf16[1,4,256,128]{3,2,1,0:T(8,128)(2,1)S(1)} collective-permute-done((bf16[1,4,256,128]{3,2,1,0:T(8,128)(2,1)S(1)}, bf16[1,4,256,128]{3,2,1,0:T(8,128)(2,1)S(1)}, u32[]{:S(2)}, u32[]{:S(2)}) %collective-permute-start.13) | collective-permute-done | bytes 262176 | tf_op jit(solution)/shard_map/ppermute | solution.py:265
  51.8 2.0 %collective-permute-start.4 = (bf16[1,4,256,128]{3,2,1,0:T(8,128)(2,1)S(1)}, bf16[1,4,256,128]{3,2,1,0:T(8,128)(2,1)S(1)}, u32[]{:S(2)}, u32[]{:S(2)}) collective-permute-start(bf16[1,4,256,128]{3,2,1,0:T(8,128)(2,1)S(1)} %get-tuple-element.33), channel_id=1, source_target_pairs={{0,16},{8,24},{16,0},{24,8},{1,17},{9,25},{17,1},{25,9},{2,18},{10... | collective-permute-start | bytes 786440 | tf_op jit(solution)/shard_map/ppermute | solution.py:265
  53.8 2.6 %collective-permute-start.12 = (bf16[1,4,256,128]{3,2,1,0:T(8,128)(2,1)S(1)}, bf16[1,4,256,128]{3,2,1,0:T(8,128)(2,1)S(1)}, u32[]{:S(2)}, u32[]{:S(2)}) collective-permute-start(bf16[1,4,256,128]{3,2,1,0:T(8,128)(2,1)S(1)} %add_blocks.16), channel_id=1, source_target_pairs={{0,4},{1,5},{2,6},{3,7},{4,0},{5,1},{6,2},{7,3},{8,12},{9,13},{10,... | collective-permute-start | bytes 786440 | tf_op jit(solution)/shard_map/ppermute | solution.py:265
  56.4 1.0 collective-permute-done.17.refs_2_
  57.4 4.1 %collective-permute-start.16 = (bf16[1,4,256,128]{3,2,1,0:T(8,128)(2,1)S(1)}, bf16[1,4,256,128]{3,2,1,0:T(8,128)(2,1)S(1)}, u32[]{:S(2)}, u32[]{:S(2)}) collective-permute-start(bf16[1,4,256,128]{3,2,1,0:T(8,128)(2,1)S(1)} %add_blocks.18), channel_id=1, source_target_pairs={{0,6},{1,7},{2,4},{3,5},{4,2},{5,3},{6,0},{7,1},{8,14},{9,15},{10,... | collective-permute-start | bytes 786440 | tf_op jit(solution)/shard_map/ppermute | solution.py:265
  61.5 1.5 %collective-permute-done.8.refs_2_ = bf16[1,4,256,128]{3,2,1,0:T(8,128)(2,1)S(1)} collective-permute-done((bf16[1,4,256,128]{3,2,1,0:T(8,128)(2,1)S(1)}, bf16[1,4,256,128]{3,2,1,0:T(8,128)(2,1)S(1)}, u32[]{:S(2)}, u32[]{:S(2)}) %collective-permute-start.8) | collective-permute-done | bytes 262176 | tf_op jit(solution)/shard_map/ppermute | solution.py:265
  63.0 2.0 %collective-permute-start.3 = (bf16[1,4,256,128]{3,2,1,0:T(8,128)(2,1)S(1)}, bf16[1,4,256,128]{3,2,1,0:T(8,128)(2,1)S(1)}, u32[]{:S(2)}, u32[]{:S(2)}) collective-permute-start(bf16[1,4,256,128]{3,2,1,0:T(8,128)(2,1)S(1)} %get-tuple-element.32), channel_id=1, source_target_pairs={{0,16},{8,24},{16,0},{24,8},{1,17},{9,25},{17,1},{25,9},{2,18},{10... | collective-permute-start | bytes 786440 | tf_op jit(solution)/shard_map/ppermute | solution.py:265
  65.1 0.8 add_blocks.17
  65.9 0.1 add_blocks.19
  66.0 0.1 add_blocks.15
  66.1 2.6 %collective-permute-done.6.refs_2_ = bf16[1,4,256,128]{3,2,1,0:T(8,128)(2,1)S(1)} collective-permute-done((bf16[1,4,256,128]{3,2,1,0:T(8,128)(2,1)S(1)}, bf16[1,4,256,128]{3,2,1,0:T(8,128)(2,1)S(1)}, u32[]{:S(2)}, u32[]{:S(2)}) %collective-permute-start.6) | collective-permute-done | bytes 262176 | tf_op jit(solution)/shard_map/ppermute | solution.py:265
  68.6 4.1 %collective-permute-start.14 = (bf16[1,4,256,128]{3,2,1,0:T(8,128)(2,1)}, bf16[1,4,256,128]{3,2,1,0:T(8,128)(2,1)}, u32[]{:S(2)}, u32[]{:S(2)}) collective-permute-start(bf16[1,4,256,128]{3,2,1,0:T(8,128)(2,1)} %add_blocks.17), channel_id=1, source_target_pairs={{0,5},{1,4},{2,7},{3,6},{4,1},{5,0},{6,3},{7,2},{8,13},{9,12},{10,... | collective-permute-start | bytes 786440 | tf_op jit(solution)/shard_map/ppermute | solution.py:265
  72.8 0.8 add_blocks.14
  73.6 0.7 collective-permute-done.4.refs_2_
  74.3 5.1 %collective-permute-start.18 = (bf16[1,4,256,128]{3,2,1,0:T(8,128)(2,1)S(1)}, bf16[1,4,256,128]{3,2,1,0:T(8,128)(2,1)}, u32[]{:S(2)}, u32[]{:S(2)}) collective-permute-start(bf16[1,4,256,128]{3,2,1,0:T(8,128)(2,1)S(1)} %add_blocks.19), channel_id=1, source_target_pairs={{0,7},{1,6},{2,5},{3,4},{4,3},{5,2},{6,1},{7,0},{8,15},{9,14},{10,... | collective-permute-start | bytes 786440 | tf_op jit(solution)/shard_map/ppermute | solution.py:265
  79.4 0.8 add_blocks.13
  80.1 3.5 %collective-permute-done.12.refs_4_ = bf16[1,4,256,128]{3,2,1,0:T(8,128)(2,1)S(1)} collective-permute-done((bf16[1,4,256,128]{3,2,1,0:T(8,128)(2,1)S(1)}, bf16[1,4,256,128]{3,2,1,0:T(8,128)(2,1)S(1)}, u32[]{:S(2)}, u32[]{:S(2)}) %collective-permute-start.12) | collective-permute-done | bytes 262176 | tf_op jit(solution)/shard_map/ppermute | solution.py:265
  83.7 0.7 copy-done
  84.4 0.2 collective-permute-start.9
  84.6 0.7 copy-done.2
  85.3 6.8 %collective-permute-start.7 = (bf16[1,4,256,128]{3,2,1,0:T(8,128)(2,1)}, bf16[1,4,256,128]{3,2,1,0:T(8,128)(2,1)}, u32[]{:S(2)}, u32[]{:S(2)}) collective-permute-start(bf16[1,4,256,128]{3,2,1,0:T(8,128)(2,1)} %add_blocks.14), channel_id=1, source_target_pairs={{0,2},{1,3},{2,0},{3,1},{4,6},{5,7},{6,4},{7,5},{8,10},{9,11},{10,... | collective-permute-start | bytes 786440 | tf_op jit(solution)/shard_map/ppermute | solution.py:265
  92.0 1.6 %collective-permute-start.5 = (bf16[1,4,256,128]{3,2,1,0:T(8,128)(2,1)}, bf16[1,4,256,128]{3,2,1,0:T(8,128)(2,1)}, u32[]{:S(2)}, u32[]{:S(2)}) collective-permute-start(bf16[1,4,256,128]{3,2,1,0:T(8,128)(2,1)} %add_blocks.13), channel_id=1, source_target_pairs={{0,1},{1,0},{2,3},{3,2},{4,5},{5,4},{6,7},{7,6},{8,9},{9,8},{10,11... | collective-permute-start | bytes 786440 | tf_op jit(solution)/shard_map/ppermute | solution.py:265
  93.6 0.1 copy.6
  93.7 0.1 reshape.9.slot_ref
  93.9 0.1 add_blocks.12.refs_0_
  94.0 3.6 %collective-permute-done.14.refs_5_ = bf16[1,4,256,128]{3,2,1,0:T(8,128)(2,1)} collective-permute-done((bf16[1,4,256,128]{3,2,1,0:T(8,128)(2,1)}, bf16[1,4,256,128]{3,2,1,0:T(8,128)(2,1)}, u32[]{:S(2)}, u32[]{:S(2)}) %collective-permute-start.14) | collective-permute-done | bytes 262176 | tf_op jit(solution)/shard_map/ppermute | solution.py:265
  97.6 0.6 collective-permute-done.9.refs_3_
  98.2 5.4 %collective-permute-done.7.refs_2_ = bf16[1,4,256,128]{3,2,1,0:T(8,128)(2,1)} collective-permute-done((bf16[1,4,256,128]{3,2,1,0:T(8,128)(2,1)}, bf16[1,4,256,128]{3,2,1,0:T(8,128)(2,1)}, u32[]{:S(2)}, u32[]{:S(2)}) %collective-permute-start.7) | collective-permute-done | bytes 262176 | tf_op jit(solution)/shard_map/ppermute | solution.py:265
  103.7 2.7 %gather_tiles.1 = bf16[1024,256]{1,0:T(8,128)(2,1)} custom-call(s32[2]{0:T(128)S(1)} %pad_add_fusion.place_ref, s32[256]{0:T(256)S(1)} %reshape.9.slot_ref, bf16[1,4,256,128]{3,2,1,0:T(8,128)(2,1)S(1)} %add_blocks.12.refs_0_, bf16[1,4,256,128]{3,2,1,0:T(8,128)(2,1)} %collective-permute-done.5.refs_1_, ...), custom_call_target="tpu_custom_call" | custom-call | tf_op jit(solution)/shard_map/gather_tiles/pallas_call | solution.py:244
  (18 shorter events, 0.1 us)
Async XLA Ops:
  0.1 0.7 copy-start.4
  19.9 2.5 %collective-permute-start = (bf16[3,4,256,128]{3,2,1,0:T(8,128)(2,1)S(1)}, bf16[3,4,256,128]{3,2,1,0:T(8,128)(2,1)S(1)}, u32[]{:S(2)}, u32[]{:S(2)}) collective-permute-start(bf16[3,4,256,128]{3,2,1,0:T(8,128)(2,1)S(1)} %get-tuple-element.25), channel_id=1, source_target_pairs={{0,8},{8,0},{16,24},{24,16},{1,9},{9,1},{17,25},{25,17},{2,10},{10... | collective-permute-start | bytes 2359304 | tf_op jit(solution)/shard_map/ppermute | solution.py:265
  29.9 3.6 %collective-permute-start.2 = (bf16[5,4,256,128]{3,2,1,0:T(8,128)(2,1)S(1)}, bf16[5,4,256,128]{3,2,1,0:T(8,128)(2,1)S(1)}, u32[]{:S(2)}, u32[]{:S(2)}) collective-permute-start(bf16[5,4,256,128]{3,2,1,0:T(8,128)(2,1)S(1)} %get-tuple-element.30), channel_id=1, source_target_pairs={{0,8},{8,0},{16,24},{24,16},{1,9},{9,1},{17,25},{25,17},{2,10},{10... | collective-permute-start | bytes 3932168 | tf_op jit(solution)/shard_map/ppermute | solution.py:265
  30.3 23.5 %collective-permute-start.1 = (bf16[5,4,256,128]{3,2,1,0:T(8,128)(2,1)S(1)}, bf16[5,4,256,128]{3,2,1,0:T(8,128)(2,1)S(1)}, u32[]{:S(2)}, u32[]{:S(2)}) collective-permute-start(bf16[5,4,256,128]{3,2,1,0:T(8,128)(2,1)S(1)} %get-tuple-element.28), channel_id=1, source_target_pairs={{0,8},{8,0},{16,24},{24,16},{1,9},{9,1},{17,25},{25,17},{2,10},{10... | collective-permute-start | bytes 3932168 | tf_op jit(solution)/shard_map/ppermute | solution.py:265
  30.4 5.7 %collective-permute-start.10 = (bf16[3,4,256,128]{3,2,1,0:T(8,128)(2,1)S(1)}, bf16[3,4,256,128]{3,2,1,0:T(8,128)(2,1)S(1)}, u32[]{:S(2)}, u32[]{:S(2)}) collective-permute-start(bf16[3,4,256,128]{3,2,1,0:T(8,128)(2,1)S(1)} %get-tuple-element.36), channel_id=1, source_target_pairs={{0,8},{8,0},{16,24},{24,16},{1,9},{9,1},{17,25},{25,17},{2,10},{10... | collective-permute-start | bytes 2359304 | tf_op jit(solution)/shard_map/ppermute | solution.py:265
  30.8 9.8 %collective-permute-start.11 = (bf16[1,4,256,128]{3,2,1,0:T(8,128)(2,1)S(1)}, bf16[1,4,256,128]{3,2,1,0:T(8,128)(2,1)S(1)}, u32[]{:S(2)}, u32[]{:S(2)}) collective-permute-start(bf16[1,4,256,128]{3,2,1,0:T(8,128)(2,1)S(1)} %get-tuple-element.27.after_ref), channel_id=1, source_target_pairs={{0,16},{8,24},{16,0},{24,8},{1,17},{9,25},{17,1},{25,9},{2,18},{10... | collective-permute-start | bytes 786440 | tf_op jit(solution)/shard_map/ppermute | solution.py:265
  33.4 12.8 %collective-permute-start.15 = (bf16[1,4,256,128]{3,2,1,0:T(8,128)(2,1)S(1)}, bf16[1,4,256,128]{3,2,1,0:T(8,128)(2,1)S(1)}, u32[]{:S(2)}, u32[]{:S(2)}) collective-permute-start(bf16[1,4,256,128]{3,2,1,0:T(8,128)(2,1)S(1)} %get-tuple-element.39), channel_id=1, source_target_pairs={{0,16},{8,24},{16,0},{24,8},{1,17},{9,25},{17,1},{25,9},{2,18},{10... | collective-permute-start | bytes 786440 | tf_op jit(solution)/shard_map/ppermute | solution.py:265
  33.4 18.4 %collective-permute-start.13 = (bf16[1,4,256,128]{3,2,1,0:T(8,128)(2,1)S(1)}, bf16[1,4,256,128]{3,2,1,0:T(8,128)(2,1)S(1)}, u32[]{:S(2)}, u32[]{:S(2)}) collective-permute-start(bf16[1,4,256,128]{3,2,1,0:T(8,128)(2,1)S(1)} %get-tuple-element.38), channel_id=1, source_target_pairs={{0,16},{8,24},{16,0},{24,8},{1,17},{9,25},{17,1},{25,9},{2,18},{10... | collective-permute-start | bytes 786440 | tf_op jit(solution)/shard_map/ppermute | solution.py:265
  36.1 21.3 %collective-permute-start.17 = (bf16[1,4,256,128]{3,2,1,0:T(8,128)(2,1)S(1)}, bf16[1,4,256,128]{3,2,1,0:T(8,128)(2,1)S(1)}, u32[]{:S(2)}, u32[]{:S(2)}) collective-permute-start(bf16[1,4,256,128]{3,2,1,0:T(8,128)(2,1)S(1)} %get-tuple-element.40), channel_id=1, source_target_pairs={{0,16},{8,24},{16,0},{24,8},{1,17},{9,25},{17,1},{25,9},{2,18},{10... | collective-permute-start | bytes 786440 | tf_op jit(solution)/shard_map/ppermute | solution.py:265
  40.6 22.5 %collective-permute-start.8 = (bf16[1,4,256,128]{3,2,1,0:T(8,128)(2,1)S(1)}, bf16[1,4,256,128]{3,2,1,0:T(8,128)(2,1)S(1)}, u32[]{:S(2)}, u32[]{:S(2)}) collective-permute-start(bf16[1,4,256,128]{3,2,1,0:T(8,128)(2,1)S(1)} %get-tuple-element.35), channel_id=1, source_target_pairs={{0,16},{8,24},{16,0},{24,8},{1,17},{9,25},{17,1},{25,9},{2,18},{10... | collective-permute-start | bytes 786440 | tf_op jit(solution)/shard_map/ppermute | solution.py:265
  46.3 22.4 %collective-permute-start.6 = (bf16[1,4,256,128]{3,2,1,0:T(8,128)(2,1)S(1)}, bf16[1,4,256,128]{3,2,1,0:T(8,128)(2,1)S(1)}, u32[]{:S(2)}, u32[]{:S(2)}) collective-permute-start(bf16[1,4,256,128]{3,2,1,0:T(8,128)(2,1)S(1)} %get-tuple-element.34), channel_id=1, source_target_pairs={{0,16},{8,24},{16,0},{24,8},{1,17},{9,25},{17,1},{25,9},{2,18},{10... | collective-permute-start | bytes 786440 | tf_op jit(solution)/shard_map/ppermute | solution.py:265
  51.8 22.5 %collective-permute-start.4 = (bf16[1,4,256,128]{3,2,1,0:T(8,128)(2,1)S(1)}, bf16[1,4,256,128]{3,2,1,0:T(8,128)(2,1)S(1)}, u32[]{:S(2)}, u32[]{:S(2)}) collective-permute-start(bf16[1,4,256,128]{3,2,1,0:T(8,128)(2,1)S(1)} %get-tuple-element.33), channel_id=1, source_target_pairs={{0,16},{8,24},{16,0},{24,8},{1,17},{9,25},{17,1},{25,9},{2,18},{10... | collective-permute-start | bytes 786440 | tf_op jit(solution)/shard_map/ppermute | solution.py:265
  53.8 29.8 %collective-permute-start.12 = (bf16[1,4,256,128]{3,2,1,0:T(8,128)(2,1)S(1)}, bf16[1,4,256,128]{3,2,1,0:T(8,128)(2,1)S(1)}, u32[]{:S(2)}, u32[]{:S(2)}) collective-permute-start(bf16[1,4,256,128]{3,2,1,0:T(8,128)(2,1)S(1)} %add_blocks.16), channel_id=1, source_target_pairs={{0,4},{1,5},{2,6},{3,7},{4,0},{5,1},{6,2},{7,3},{8,12},{9,13},{10,... | collective-permute-start | bytes 786440 | tf_op jit(solution)/shard_map/ppermute | solution.py:265
  57.4 27.2 %collective-permute-start.16 = (bf16[1,4,256,128]{3,2,1,0:T(8,128)(2,1)S(1)}, bf16[1,4,256,128]{3,2,1,0:T(8,128)(2,1)S(1)}, u32[]{:S(2)}, u32[]{:S(2)}) collective-permute-start(bf16[1,4,256,128]{3,2,1,0:T(8,128)(2,1)S(1)} %add_blocks.18), channel_id=1, source_target_pairs={{0,6},{1,7},{2,4},{3,5},{4,2},{5,3},{6,0},{7,1},{8,14},{9,15},{10,... | collective-permute-start | bytes 786440 | tf_op jit(solution)/shard_map/ppermute | solution.py:265
  63.0 29.0 %collective-permute-start.3 = (bf16[1,4,256,128]{3,2,1,0:T(8,128)(2,1)S(1)}, bf16[1,4,256,128]{3,2,1,0:T(8,128)(2,1)S(1)}, u32[]{:S(2)}, u32[]{:S(2)}) collective-permute-start(bf16[1,4,256,128]{3,2,1,0:T(8,128)(2,1)S(1)} %get-tuple-element.32), channel_id=1, source_target_pairs={{0,16},{8,24},{16,0},{24,8},{1,17},{9,25},{17,1},{25,9},{2,18},{10... | collective-permute-start | bytes 786440 | tf_op jit(solution)/shard_map/ppermute | solution.py:265
  68.6 28.9 %collective-permute-start.14 = (bf16[1,4,256,128]{3,2,1,0:T(8,128)(2,1)}, bf16[1,4,256,128]{3,2,1,0:T(8,128)(2,1)}, u32[]{:S(2)}, u32[]{:S(2)}) collective-permute-start(bf16[1,4,256,128]{3,2,1,0:T(8,128)(2,1)} %add_blocks.17), channel_id=1, source_target_pairs={{0,5},{1,4},{2,7},{3,6},{4,1},{5,0},{6,3},{7,2},{8,13},{9,12},{10,... | collective-permute-start | bytes 786440 | tf_op jit(solution)/shard_map/ppermute | solution.py:265
  73.6 20.0 %copy-start.5 = (s32[8,8,4]{1,2,0:T(4,128)S(1)}, s32[8,8,4]{1,2,0:T(4,128)}, u32[]{:S(2)}) copy-start(s32[8,8,4]{1,2,0:T(4,128)} %param.9) | copy-start | bytes 3076
  74.3 23.3 %collective-permute-start.18 = (bf16[1,4,256,128]{3,2,1,0:T(8,128)(2,1)S(1)}, bf16[1,4,256,128]{3,2,1,0:T(8,128)(2,1)}, u32[]{:S(2)}, u32[]{:S(2)}) collective-permute-start(bf16[1,4,256,128]{3,2,1,0:T(8,128)(2,1)S(1)} %add_blocks.19), channel_id=1, source_target_pairs={{0,7},{1,6},{2,5},{3,4},{4,3},{5,2},{6,1},{7,0},{8,15},{9,14},{10,... | collective-permute-start | bytes 786440 | tf_op jit(solution)/shard_map/ppermute | solution.py:265
  83.7 0.7 copy-start
  84.4 13.8 %collective-permute-start.9 = (bf16[1,4,256,128]{3,2,1,0:T(8,128)(2,1)S(1)}, bf16[1,4,256,128]{3,2,1,0:T(8,128)(2,1)}, u32[]{:S(2)}, u32[]{:S(2)}) collective-permute-start(bf16[1,4,256,128]{3,2,1,0:T(8,128)(2,1)S(1)} %add_blocks.15), channel_id=1, source_target_pairs={{0,3},{1,2},{2,1},{3,0},{4,7},{5,6},{6,5},{7,4},{8,11},{9,10},{10,... | collective-permute-start | bytes 786440 | tf_op jit(solution)/shard_map/ppermute | solution.py:265
  84.6 0.7 copy-start.2
  85.3 18.4 %collective-permute-start.7 = (bf16[1,4,256,128]{3,2,1,0:T(8,128)(2,1)}, bf16[1,4,256,128]{3,2,1,0:T(8,128)(2,1)}, u32[]{:S(2)}, u32[]{:S(2)}) collective-permute-start(bf16[1,4,256,128]{3,2,1,0:T(8,128)(2,1)} %add_blocks.14), channel_id=1, source_target_pairs={{0,2},{1,3},{2,0},{3,1},{4,6},{5,7},{6,4},{7,5},{8,10},{9,11},{10,... | collective-permute-start | bytes 786440 | tf_op jit(solution)/shard_map/ppermute | solution.py:265
  92.0 11.6 %collective-permute-start.5 = (bf16[1,4,256,128]{3,2,1,0:T(8,128)(2,1)}, bf16[1,4,256,128]{3,2,1,0:T(8,128)(2,1)}, u32[]{:S(2)}, u32[]{:S(2)}) collective-permute-start(bf16[1,4,256,128]{3,2,1,0:T(8,128)(2,1)} %add_blocks.13), channel_id=1, source_target_pairs={{0,1},{1,0},{2,3},{3,2},{4,5},{5,4},{6,7},{7,6},{8,9},{9,8},{10,11... | collective-permute-start | bytes 786440 | tf_op jit(solution)/shard_map/ppermute | solution.py:265
  93.8 9.8 %copy-start.1 = (bf16[1,4,256,128]{3,2,1,0:T(8,128)(2,1)S(1)}, bf16[1,4,256,128]{3,2,1,0:T(8,128)(2,1)}, u32[]{:S(2)}) copy-start(bf16[1,4,256,128]{3,2,1,0:T(8,128)(2,1)} %copy-done) | copy-start | bytes 786436
  93.9 9.8 %copy-start.3 = (bf16[1,4,256,128]{3,2,1,0:T(8,128)(2,1)S(1)}, bf16[1,4,256,128]{3,2,1,0:T(8,128)(2,1)}, u32[]{:S(2)}) copy-start(bf16[1,4,256,128]{3,2,1,0:T(8,128)(2,1)} %copy-done.2) | copy-start | bytes 786436
where the time goes:
time: 107 us; the launch traced here: 106 us
  starting transfers between devices  41.7 us (39%)
  Pallas kernels  32.7 us (31%)
  waiting for transfers between devices  29.5 us (28%)
  local copies, waits for them, and re-layouts  2.28 us (2%)
    ppermute x19, starting transfers between devices, swap(): lax.ppermute(array, axis, [(i, i ^ bit) for i in range(lax.axis_size(axis...  41.7 us
    ppermute x19, waiting for transfers between devices, swap(): lax.ppermute(array, axis, [(i, i ^ bit) for i in range(lax.axis_size(axis...  29.5 us
    pallas_call x1, Pallas kernels, first_products(): pl.pallas_call(functools.partial(first_kernel, groups=groups), grid_spec=...  19.2 us
    pallas_call x1, Pallas kernels, rest_products(): pl.pallas_call(rest_kernel, grid_spec=pltpu.PrefetchScalarGridSpec(num_sc...  7.31 us
    pallas_call x10, Pallas kernels, add_blocks(): pl.pallas_call(functools.partial(add_kernel, plan=tuple(plan)), in_specs=...  3.44 us
    pallas_call x1, Pallas kernels, gather_tiles(): pl.pallas_call(gather_kernel, in_specs=[scalars, scalars] + [spec for _ i...  2.74 us
    unnamed x13, local copies, waits for them, and re-layouts  2.17 us
  transfers between devices with their start and end apart: 19, of which 12 were waited for; matrix products, arithmetic and copies ran while one was open for 0% of the time, Pallas kernels for 3%

commit v1 on v0

--- a/solution.py
+++ b/solution.py
@@ -16,7 +16,7 @@
 BLOCK = 128
 SIDE = 64
 CHUNKS = 8
-EARLY = 3
+EDGES = (0, 2, 4, 8)
 
 
 def fill_coef(scale_ref, cells_ref, codes_ref, write, low_ref, high_ref, weight_ref, table_ref):
@@ -159,9 +159,9 @@
     put_products(flip_ref[...], coef_ref[...], out_refs)
 
 
-def rest_products(place, coef, flip, after, replicas, width, capacity, groups, first):
+def rest_products(place, coef, flip, after, replicas, width, capacity, groups, first, stop):
     tokens = coef.shape[0]
-    length = groups - first
+    length = stop - first
     return pl.pallas_call(
         rest_kernel,
         grid_spec=pltpu.PrefetchScalarGridSpec(
@@ -266,39 +266,41 @@
 
     chunks = min(CHUNKS, groups)
     size = groups // chunks
-    early = max(1, EARLY * chunks // CHUNKS) * size
+    edges = sorted({max(edge and 1, edge * chunks // CHUNKS) for edge in EDGES})
     pieces = [{m: [] for m in range(0, replicas, 2)} for _ in range(chunks)]
-
-    def take(outs, first):
-        order = sorted(range(replicas), reverse=True)
-        for m in order:
+    sent = None
+    for stage, (first, stop) in enumerate(zip(edges, edges[1:])):
+        if stage == 0:
+            coef, flip, *outs = first_products(
+                place,
+                head_scale,
+                by_pair(pair_cells),
+                by_pair(weight_codes),
+                out_grad,
+                replicas,
+                width,
+                capacity,
+                groups,
+                stop * size,
+            )
+        else:
+            outs = rest_products(place, coef, flip, sent, replicas, width, capacity, groups, first * size, stop * size)
+        for m in sorted(range(replicas), reverse=True):
             array = swap(outs[m], "dp", 1) if m & 1 else outs[m]
-            for n in range(array.shape[0] // size):
-                pieces[first // size + n][m & ~1].append((array, n))
-
-    def send_far(first, stop):
+            for n in range(first, stop):
+                pieces[n][m & ~1].append((array, n - first))
         some = pieces[first:stop]
+        sent = outs[0]
         bit = 2
-        sent = None
         while bit < replicas:
             masks = [m for m in sorted(some[0], reverse=True) if m & bit]
-            sums = iter(add_blocks([piece.pop(m) for piece in some for m in masks], size))
-            for piece in some:
+            sums = add_blocks([piece.pop(m) for piece in some for m in masks], size)
+            sent = sums[0] if bit == 2 else sent
+            sums = iter(sums)
+            for n, piece in enumerate(some, first):
                 for m in masks:
-                    total = next(sums)
-                    sent = total if sent is None else sent
-                    piece[m ^ bit].append((swap(total, "dp", bit), 0))
+                    piece[m ^ bit].append((swap(next(sums), "dp", bit), 0))
             bit *= 2
-        return sent
-
-    coef, flip, *outs = first_products(
-        place, head_scale, by_pair(pair_cells), by_pair(weight_codes), out_grad, replicas, width, capacity, groups, early
-    )
-    take(outs, 0)
-    sent = send_far(0, early // size)
-    outs = rest_products(place, coef, flip, outs[0] if sent is None else sent, replicas, width, capacity, groups, early)
-    take(outs, early)
-    send_far(early // size, chunks)
     parts = {}
     for chunk, piece in enumerate(pieces):
         (mine,) = add_blocks([piece[0]], size)

time: 107 us -> 116 us (1.084); the launches traced: 106 us -> 114 us
  waiting for transfers between devices: 29.5 us -> 46.9 us
  starting transfers between devices: 41.7 us -> 32.6 us
    ppermute x19 -> x21, waiting for transfers between devices: 29.5 us -> 46.9 us  [swap(): lax.ppermute(array, axis, [(i, i ^ bit) for i in range(lax.axis_size(axis...]
    ppermute x19 -> x21, starting transfers between devices: 41.7 us -> 32.6 us  [swap(): lax.ppermute(array, axis, [(i, i ^ bit) for i in range(lax.axis_size(axis...]
    pallas_call x1 -> x2, Pallas kernels: 7.31 us -> 9.23 us  [rest_products(): pl.pallas_call(rest_kernel, grid_spec=pltpu.PrefetchScalarGridSpec(num_sc...]
    pallas_call x10 -> x11, Pallas kernels: 3.44 us -> 2.01 us  [add_blocks(): pl.pallas_call(functools.partial(add_kernel, plan=tuple(plan)), in_specs=...]
    pallas_call x1, Pallas kernels: 19.2 us -> 17.8 us  [first_products(): pl.pallas_call(functools.partial(first_kernel, groups=groups), grid_spec=...]
  transfers between devices with their start and end apart: 19 -> 21, of which waited for: 12 -> 14; matrix products, arithmetic and copies ran while one was open for 0% -> 0% of each run, Pallas kernels for 3% -> 2%
where the time goes in v1:
time: 116 us; the launch traced here: 114 us
  waiting for transfers between devices  46.9 us (40%)
  starting transfers between devices  32.6 us (28%)
  Pallas kernels  31.8 us (27%)
  local copies, waits for them, and re-layouts  2.34 us (2%)
    ppermute x21, waiting for transfers between devices, swap(): lax.ppermute(array, axis, [(i, i ^ bit) for i in range(lax.axis_size(axis...  46.9 us
    ppermute x21, starting transfers between devices, swap(): lax.ppermute(array, axis, [(i, i ^ bit) for i in range(lax.axis_size(axis...  32.6 us
    pallas_call x1, Pallas kernels, first_products(): pl.pallas_call(functools.partial(first_kernel, groups=groups), grid_spec=...  17.8 us
    pallas_call x2, Pallas kernels, rest_products(): pl.pallas_call(rest_kernel, grid_spec=pltpu.PrefetchScalarGridSpec(num_sc...  9.23 us
    pallas_call x1, Pallas kernels, gather_tiles(): pl.pallas_call(gather_kernel, in_specs=[scalars, scalars] + [spec for _ i...  2.73 us
  transfers between devices with their start and end apart: 21, of which 14 were waited for; matrix products, arithmetic and copies ran while one was open for 0% of the time, Pallas kernels for 2%

profile of v1, /device:TPU:0, one launch (start us, length us, event | category | flops | bytes accessed | tf_op | source)
XLA Modules:
  0.0 113.9 jit_solution(8400229465070572213)
XLA Ops:
  0.1 0.7 copy-done.4
  0.7 17.8 %first_products.1 = (bf16[1024,4096]{1,0:T(8,128)(2,1)S(1)}, bf16[1024,1024]{1,0:T(8,128)(2,1)S(1)}, bf16[2,4,256,128]{3,2,1,0:T(8,128)(2,1)S(1)}, bf16[2,4,256,...) custom-call(s32[2]{0:T(128)S(1)} %pad_add_fusion.place_ref, ...), custom_call_target="tpu_custom_call" | custom-call | flops 8589934592 | bytes 16777216 | tf_op jit(solution)/shard_map/first_products/pallas_call | solution.py:120
  18.6 0.5 collective-permute-start
  19.1 1.5 %collective-permute-done.refs_0_ = bf16[2,4,256,128]{3,2,1,0:T(8,128)(2,1)S(1)} collective-permute-done((bf16[2,4,256,128]{3,2,1,0:T(8,128)(2,1)S(1)}, bf16[2,4,256,128]{3,2,1,0:T(8,128)(2,1)S(1)}, u32[]{:S(2)}, u32[]{:S(2)}) %collective-permute-start) | collective-permute-done | bytes 524320 | tf_op jit(solution)/shard_map/ppermute | solution.py:265
  20.6 0.1 add_blocks.11
  20.8 3.3 %rest_products.2 = (bf16[2,4,256,128]{3,2,1,0:T(8,128)(2,1)S(1)}, bf16[2,4,256,128]{3,2,1,0:T(8,128)(2,1)S(1)}, bf16[2,4,256,128]{3,2,1,0:T(8,128)(2,1)S(1)}, bf16[2,4,256,128]{3,2,1,0:T(8,128)(2,1)S(1)}) custom-call(s32[2]{0:T(128)S(1)} %pad_add_fusion.place_ref, bf16[1024,4096]{1,0:T(8,128)(2,1)S(1)} %get-tuple-element.27.coef_ref, ...), custom_call_target="tpu_custom_call" | custom-call | flops 2147483648 | bytes 6291456 | tf_op jit(solution)/shard_map/rest_products/pallas_call | solution.py:165
  24.0 0.4 collective-permute-start.1
  24.5 1.5 %collective-permute-done.1.refs_0_ = bf16[2,4,256,128]{3,2,1,0:T(8,128)(2,1)S(1)} collective-permute-done((bf16[2,4,256,128]{3,2,1,0:T(8,128)(2,1)S(1)}, bf16[2,4,256,128]{3,2,1,0:T(8,128)(2,1)S(1)}, u32[]{:S(2)}, u32[]{:S(2)}) %collective-permute-start.1) | collective-permute-done | bytes 524320 | tf_op jit(solution)/shard_map/ppermute | solution.py:265
  26.0 0.1 add_blocks.12
  26.2 6.0 %rest_products.3 = (bf16[4,4,256,128]{3,2,1,0:T(8,128)(2,1)S(1)}, bf16[4,4,256,128]{3,2,1,0:T(8,128)(2,1)S(1)}, bf16[4,4,256,128]{3,2,1,0:T(8,128)(2,1)S(1)}, bf16[4,4,256,128]{3,2,1,0:T(8,128)(2,1)S(1)}) custom-call(s32[2]{0:T(128)S(1)} %pad_add_fusion.place_ref, bf16[1024,4096]{1,0:T(8,128)(2,1)S(1)} %get-tuple-element.27.coef_ref, ...), custom_call_target="tpu_custom_call" | custom-call | flops 4294967296 | bytes 10485760 | tf_op jit(solution)/shard_map/rest_products/pallas_call | solution.py:165
  32.1 0.4 collective-permute-start.3
  32.6 0.2 collective-permute-start.11
  32.7 0.4 collective-permute-start.2
  33.1 0.2 collective-permute-start.16
  33.2 2.8 %collective-permute-start.14 = (bf16[1,4,256,128]{3,2,1,0:T(8,128)(2,1)S(1)}, bf16[1,4,256,128]{3,2,1,0:T(8,128)(2,1)S(1)}, u32[]{:S(2)}, u32[]{:S(2)}) collective-permute-start(bf16[1,4,256,128]{3,2,1,0:T(8,128)(2,1)S(1)} %get-tuple-element.45), channel_id=1, source_target_pairs={{0,16},{8,24},{16,0},{24,8},{1,17},{9,25},{17,1},{25,9},{2,18},{10... | collective-permute-start | bytes 786440 | tf_op jit(solution)/shard_map/ppermute | solution.py:265
  36.1 2.4 %collective-permute-start.12 = (bf16[1,4,256,128]{3,2,1,0:T(8,128)(2,1)S(1)}, bf16[1,4,256,128]{3,2,1,0:T(8,128)(2,1)S(1)}, u32[]{:S(2)}, u32[]{:S(2)}) collective-permute-start(bf16[1,4,256,128]{3,2,1,0:T(8,128)(2,1)S(1)} %get-tuple-element.31.after_ref), channel_id=1, source_target_pairs={{0,16},{8,24},{16,0},{24,8},{1,17},{9,25},{17,1},{25,9},{2,18},{10... | collective-permute-start | bytes 786440 | tf_op jit(solution)/shard_map/ppermute | solution.py:265
  38.4 4.8 %collective-permute-done.14.refs_2_ = bf16[1,4,256,128]{3,2,1,0:T(8,128)(2,1)S(1)} collective-permute-done((bf16[1,4,256,128]{3,2,1,0:T(8,128)(2,1)S(1)}, bf16[1,4,256,128]{3,2,1,0:T(8,128)(2,1)S(1)}, u32[]{:S(2)}, u32[]{:S(2)}) %collective-permute-start.14) | collective-permute-done | bytes 262176 | tf_op jit(solution)/shard_map/ppermute | solution.py:265
  43.2 2.0 %collective-permute-start.19 = (bf16[1,4,256,128]{3,2,1,0:T(8,128)(2,1)S(1)}, bf16[1,4,256,128]{3,2,1,0:T(8,128)(2,1)S(1)}, u32[]{:S(2)}, u32[]{:S(2)}) collective-permute-start(bf16[1,4,256,128]{3,2,1,0:T(8,128)(2,1)S(1)} %get-tuple-element.48), channel_id=1, source_target_pairs={{0,16},{8,24},{16,0},{24,8},{1,17},{9,25},{17,1},{25,9},{2,18},{10... | collective-permute-start | bytes 786440 | tf_op jit(solution)/shard_map/ppermute | solution.py:265
  45.3 0.3 add_blocks.13
  45.5 3.3 %collective-permute-done.12.refs_2_ = bf16[1,4,256,128]{3,2,1,0:T(8,128)(2,1)S(1)} collective-permute-done((bf16[1,4,256,128]{3,2,1,0:T(8,128)(2,1)S(1)}, bf16[1,4,256,128]{3,2,1,0:T(8,128)(2,1)S(1)}, u32[]{:S(2)}, u32[]{:S(2)}) %collective-permute-start.12) | collective-permute-done | bytes 262176 | tf_op jit(solution)/shard_map/ppermute | solution.py:265
  48.8 2.0 %collective-permute-start.5 = (bf16[1,4,256,128]{3,2,1,0:T(8,128)(2,1)S(1)}, bf16[1,4,256,128]{3,2,1,0:T(8,128)(2,1)S(1)}, u32[]{:S(2)}, u32[]{:S(2)}) collective-permute-start(bf16[1,4,256,128]{3,2,1,0:T(8,128)(2,1)S(1)} %get-tuple-element.40), channel_id=1, source_target_pairs={{0,16},{8,24},{16,0},{24,8},{1,17},{9,25},{17,1},{25,9},{2,18},{10... | collective-permute-start | bytes 786440 | tf_op jit(solution)/shard_map/ppermute | solution.py:265
  50.8 0.1 add_blocks.19
  50.9 0.1 add_blocks.18
  51.1 3.3 %collective-permute-done.19.refs_2_ = bf16[1,4,256,128]{3,2,1,0:T(8,128)(2,1)S(1)} collective-permute-done((bf16[1,4,256,128]{3,2,1,0:T(8,128)(2,1)S(1)}, bf16[1,4,256,128]{3,2,1,0:T(8,128)(2,1)S(1)}, u32[]{:S(2)}, u32[]{:S(2)}) %collective-permute-start.19) | collective-permute-done | bytes 262176 | tf_op jit(solution)/shard_map/ppermute | solution.py:265
  54.4 2.0 %collective-permute-start.9 = (bf16[1,4,256,128]{3,2,1,0:T(8,128)(2,1)S(1)}, bf16[1,4,256,128]{3,2,1,0:T(8,128)(2,1)S(1)}, u32[]{:S(2)}, u32[]{:S(2)}) collective-permute-start(bf16[1,4,256,128]{3,2,1,0:T(8,128)(2,1)S(1)} %get-tuple-element.42), channel_id=1, source_target_pairs={{0,16},{8,24},{16,0},{24,8},{1,17},{9,25},{17,1},{25,9},{2,18},{10... | collective-permute-start | bytes 786440 | tf_op jit(solution)/shard_map/ppermute | solution.py:265
  56.5 3.6 %collective-permute-done.17.refs_2_ = bf16[1,4,256,128]{3,2,1,0:T(8,128)(2,1)S(1)} collective-permute-done((bf16[1,4,256,128]{3,2,1,0:T(8,128)(2,1)S(1)}, bf16[1,4,256,128]{3,2,1,0:T(8,128)(2,1)S(1)}, u32[]{:S(2)}, u32[]{:S(2)}) %collective-permute-start.17) | collective-permute-done | bytes 262176 | tf_op jit(solution)/shard_map/ppermute | solution.py:265
  60.1 3.1 %collective-permute-start.13 = (bf16[1,4,256,128]{3,2,1,0:T(8,128)(2,1)S(1)}, bf16[1,4,256,128]{3,2,1,0:T(8,128)(2,1)S(1)}, u32[]{:S(2)}, u32[]{:S(2)}) collective-permute-start(bf16[1,4,256,128]{3,2,1,0:T(8,128)(2,1)S(1)} %add_blocks.18), channel_id=1, source_target_pairs={{0,4},{1,5},{2,6},{3,7},{4,0},{5,1},{6,2},{7,3},{8,12},{9,13},{10,... | collective-permute-start | bytes 786440 | tf_op jit(solution)/shard_map/ppermute | solution.py:265
  63.2 1.3 %collective-permute-start.15 = (bf16[1,4,256,128]{3,2,1,0:T(8,128)(2,1)S(1)}, bf16[1,4,256,128]{3,2,1,0:T(8,128)(2,1)S(1)}, u32[]{:S(2)}, u32[]{:S(2)}) collective-permute-start(bf16[1,4,256,128]{3,2,1,0:T(8,128)(2,1)S(1)} %add_blocks.19), channel_id=1, source_target_pairs={{0,5},{1,4},{2,7},{3,6},{4,1},{5,0},{6,3},{7,2},{8,13},{9,12},{10,... | collective-permute-start | bytes 786440 | tf_op jit(solution)/shard_map/ppermute | solution.py:265
  64.5 1.2 %collective-permute-done.5.refs_2_ = bf16[1,4,256,128]{3,2,1,0:T(8,128)(2,1)S(1)} collective-permute-done((bf16[1,4,256,128]{3,2,1,0:T(8,128)(2,1)S(1)}, bf16[1,4,256,128]{3,2,1,0:T(8,128)(2,1)S(1)}, u32[]{:S(2)}, u32[]{:S(2)}) %collective-permute-start.5) | collective-permute-done | bytes 262176 | tf_op jit(solution)/shard_map/ppermute | solution.py:265
  65.7 2.0 %collective-permute-start.4 = (bf16[1,4,256,128]{3,2,1,0:T(8,128)(2,1)S(1)}, bf16[1,4,256,128]{3,2,1,0:T(8,128)(2,1)S(1)}, u32[]{:S(2)}, u32[]{:S(2)}) collective-permute-start(bf16[1,4,256,128]{3,2,1,0:T(8,128)(2,1)S(1)} %get-tuple-element.39), channel_id=1, source_target_pairs={{0,16},{8,24},{16,0},{24,8},{1,17},{9,25},{17,1},{25,9},{2,18},{10... | collective-permute-start | bytes 786440 | tf_op jit(solution)/shard_map/ppermute | solution.py:265
  67.8 0.8 add_blocks.20
  68.7 2.6 %collective-permute-done.7.refs_2_ = bf16[1,4,256,128]{3,2,1,0:T(8,128)(2,1)S(1)} collective-permute-done((bf16[1,4,256,128]{3,2,1,0:T(8,128)(2,1)S(1)}, bf16[1,4,256,128]{3,2,1,0:T(8,128)(2,1)S(1)}, u32[]{:S(2)}, u32[]{:S(2)}) %collective-permute-start.7) | collective-permute-done | bytes 262176 | tf_op jit(solution)/shard_map/ppermute | solution.py:265
  71.3 4.1 %collective-permute-start.18 = (bf16[1,4,256,128]{3,2,1,0:T(8,128)(2,1)}, bf16[1,4,256,128]{3,2,1,0:T(8,128)(2,1)}, u32[]{:S(2)}, u32[]{:S(2)}) collective-permute-start(bf16[1,4,256,128]{3,2,1,0:T(8,128)(2,1)} %add_blocks.20), channel_id=1, source_target_pairs={{0,6},{1,7},{2,4},{3,5},{4,2},{5,3},{6,0},{7,1},{8,14},{9,15},{10,... | collective-permute-start | bytes 786440 | tf_op jit(solution)/shard_map/ppermute | solution.py:265
  75.5 1.4 %collective-permute-done.9.refs_2_ = bf16[1,4,256,128]{3,2,1,0:T(8,128)(2,1)S(1)} collective-permute-done((bf16[1,4,256,128]{3,2,1,0:T(8,128)(2,1)S(1)}, bf16[1,4,256,128]{3,2,1,0:T(8,128)(2,1)S(1)}, u32[]{:S(2)}, u32[]{:S(2)}) %collective-permute-start.9) | collective-permute-done | bytes 262176 | tf_op jit(solution)/shard_map/ppermute | solution.py:265
  76.9 5.1 %collective-permute-start.20 = (bf16[1,4,256,128]{3,2,1,0:T(8,128)(2,1)S(1)}, bf16[1,4,256,128]{3,2,1,0:T(8,128)(2,1)}, u32[]{:S(2)}, u32[]{:S(2)}) collective-permute-start(bf16[1,4,256,128]{3,2,1,0:T(8,128)(2,1)S(1)} %add_blocks.21), channel_id=1, source_target_pairs={{0,7},{1,6},{2,5},{3,4},{4,3},{5,2},{6,1},{7,0},{8,15},{9,14},{10,... | collective-permute-start | bytes 786440 | tf_op jit(solution)/shard_map/ppermute | solution.py:265
  82.1 9.6 %collective-permute-done.13.refs_4_ = bf16[1,4,256,128]{3,2,1,0:T(8,128)(2,1)S(1)} collective-permute-done((bf16[1,4,256,128]{3,2,1,0:T(8,128)(2,1)S(1)}, bf16[1,4,256,128]{3,2,1,0:T(8,128)(2,1)S(1)}, u32[]{:S(2)}, u32[]{:S(2)}) %collective-permute-start.13) | collective-permute-done | bytes 262176 | tf_op jit(solution)/shard_map/ppermute | solution.py:265
  91.8 0.7 copy-done
  92.5 1.5 %collective-permute-start.6 = (bf16[1,4,256,128]{3,2,1,0:T(8,128)(2,1)S(1)}, bf16[1,4,256,128]{3,2,1,0:T(8,128)(2,1)}, u32[]{:S(2)}, u32[]{:S(2)}) collective-permute-start(bf16[1,4,256,128]{3,2,1,0:T(8,128)(2,1)S(1)} %add_blocks.15), channel_id=1, source_target_pairs={{0,1},{1,0},{2,3},{3,2},{4,5},{5,4},{6,7},{7,6},{8,9},{9,8},{10,11... | collective-permute-start | bytes 786440 | tf_op jit(solution)/shard_map/ppermute | solution.py:265
  94.0 4.3 %collective-permute-done.15.refs_5_ = bf16[1,4,256,128]{3,2,1,0:T(8,128)(2,1)S(1)} collective-permute-done((bf16[1,4,256,128]{3,2,1,0:T(8,128)(2,1)S(1)}, bf16[1,4,256,128]{3,2,1,0:T(8,128)(2,1)S(1)}, u32[]{:S(2)}, u32[]{:S(2)}) %collective-permute-start.15) | collective-permute-done | bytes 262176 | tf_op jit(solution)/shard_map/ppermute | solution.py:265
  98.3 0.7 copy-done.2
  99.1 2.0 %collective-permute-start.10 = (bf16[1,4,256,128]{3,2,1,0:T(8,128)(2,1)S(1)}, bf16[1,4,256,128]{3,2,1,0:T(8,128)(2,1)}, u32[]{:S(2)}, u32[]{:S(2)}) collective-permute-start(bf16[1,4,256,128]{3,2,1,0:T(8,128)(2,1)S(1)} %add_blocks.17), channel_id=1, source_target_pairs={{0,3},{1,2},{2,1},{3,0},{4,7},{5,6},{6,5},{7,4},{8,11},{9,10},{10,... | collective-permute-start | bytes 786440 | tf_op jit(solution)/shard_map/ppermute | solution.py:265
  101.0 0.1 copy.6
  101.2 0.1 reshape.9.slot_ref
  101.3 0.1 add_blocks.14.refs_0_
  101.4 2.2 %collective-permute-done.6.refs_1_ = bf16[1,4,256,128]{3,2,1,0:T(8,128)(2,1)} collective-permute-done((bf16[1,4,256,128]{3,2,1,0:T(8,128)(2,1)S(1)}, bf16[1,4,256,128]{3,2,1,0:T(8,128)(2,1)}, u32[]{:S(2)}, u32[]{:S(2)}) %collective-permute-start.6) | collective-permute-done | bytes 262176 | tf_op jit(solution)/shard_map/ppermute | solution.py:265
  103.7 4.4 %collective-permute-done.8.refs_2_ = bf16[1,4,256,128]{3,2,1,0:T(8,128)(2,1)} collective-permute-done((bf16[1,4,256,128]{3,2,1,0:T(8,128)(2,1)S(1)}, bf16[1,4,256,128]{3,2,1,0:T(8,128)(2,1)}, u32[]{:S(2)}, u32[]{:S(2)}) %collective-permute-start.8) | collective-permute-done | bytes 262176 | tf_op jit(solution)/shard_map/ppermute | solution.py:265
  108.1 3.1 %collective-permute-done.10.refs_3_ = bf16[1,4,256,128]{3,2,1,0:T(8,128)(2,1)} collective-permute-done((bf16[1,4,256,128]{3,2,1,0:T(8,128)(2,1)S(1)}, bf16[1,4,256,128]{3,2,1,0:T(8,128)(2,1)}, u32[]{:S(2)}, u32[]{:S(2)}) %collective-permute-start.10) | collective-permute-done | bytes 262176 | tf_op jit(solution)/shard_map/ppermute | solution.py:265
  111.2 2.7 %gather_tiles.1 = bf16[1024,256]{1,0:T(8,128)(2,1)} custom-call(s32[2]{0:T(128)S(1)} %pad_add_fusion.place_ref, s32[256]{0:T(256)S(1)} %reshape.9.slot_ref, bf16[1,4,256,128]{3,2,1,0:T(8,128)(2,1)S(1)} %add_blocks.14.refs_0_, bf16[1,4,256,128]{3,2,1,0:T(8,128)(2,1)} %collective-permute-done.6.refs_1_, ...), custom_call_target="tpu_custom_call" | custom-call | tf_op jit(solution)/shard_map/gather_tiles/pallas_call | solution.py:244
  (24 shorter events, 0.6 us)
Async XLA Ops:
  0.1 0.7 copy-start.4
  18.6 2.1 %collective-permute-start = (bf16[2,4,256,128]{3,2,1,0:T(8,128)(2,1)S(1)}, bf16[2,4,256,128]{3,2,1,0:T(8,128)(2,1)S(1)}, u32[]{:S(2)}, u32[]{:S(2)}) collective-permute-start(bf16[2,4,256,128]{3,2,1,0:T(8,128)(2,1)S(1)} %get-tuple-element.29), channel_id=1, source_target_pairs={{0,8},{8,0},{16,24},{24,16},{1,9},{9,1},{17,25},{25,17},{2,10},{10... | collective-permute-start | bytes 1572872 | tf_op jit(solution)/shard_map/ppermute | solution.py:265
  24.0 2.0 %collective-permute-start.1 = (bf16[2,4,256,128]{3,2,1,0:T(8,128)(2,1)S(1)}, bf16[2,4,256,128]{3,2,1,0:T(8,128)(2,1)S(1)}, u32[]{:S(2)}, u32[]{:S(2)}) collective-permute-start(bf16[2,4,256,128]{3,2,1,0:T(8,128)(2,1)S(1)} %get-tuple-element.32), channel_id=1, source_target_pairs={{0,8},{8,0},{16,24},{24,16},{1,9},{9,1},{17,25},{25,17},{2,10},{10... | collective-permute-start | bytes 1572872 | tf_op jit(solution)/shard_map/ppermute | solution.py:265
  32.1 13.1 %collective-permute-start.3 = (bf16[4,4,256,128]{3,2,1,0:T(8,128)(2,1)S(1)}, bf16[4,4,256,128]{3,2,1,0:T(8,128)(2,1)S(1)}, u32[]{:S(2)}, u32[]{:S(2)}) collective-permute-start(bf16[4,4,256,128]{3,2,1,0:T(8,128)(2,1)S(1)} %get-tuple-element.37), channel_id=1, source_target_pairs={{0,8},{8,0},{16,24},{24,16},{1,9},{9,1},{17,25},{25,17},{2,10},{10... | collective-permute-start | bytes 3145736 | tf_op jit(solution)/shard_map/ppermute | solution.py:265
  32.6 3.5 %collective-permute-start.11 = (bf16[2,4,256,128]{3,2,1,0:T(8,128)(2,1)S(1)}, bf16[2,4,256,128]{3,2,1,0:T(8,128)(2,1)S(1)}, u32[]{:S(2)}, u32[]{:S(2)}) collective-permute-start(bf16[2,4,256,128]{3,2,1,0:T(8,128)(2,1)S(1)} %get-tuple-element.43), channel_id=1, source_target_pairs={{0,8},{8,0},{16,24},{24,16},{1,9},{9,1},{17,25},{25,17},{2,10},{10... | collective-permute-start | bytes 1572872 | tf_op jit(solution)/shard_map/ppermute | solution.py:265
  32.7 30.5 %collective-permute-start.2 = (bf16[4,4,256,128]{3,2,1,0:T(8,128)(2,1)S(1)}, bf16[4,4,256,128]{3,2,1,0:T(8,128)(2,1)S(1)}, u32[]{:S(2)}, u32[]{:S(2)}) collective-permute-start(bf16[4,4,256,128]{3,2,1,0:T(8,128)(2,1)S(1)} %get-tuple-element.35), channel_id=1, source_target_pairs={{0,8},{8,0},{16,24},{24,16},{1,9},{9,1},{17,25},{25,17},{2,10},{10... | collective-permute-start | bytes 3145736 | tf_op jit(solution)/shard_map/ppermute | solution.py:265
  33.1 18.0 %collective-permute-start.16 = (bf16[2,4,256,128]{3,2,1,0:T(8,128)(2,1)S(1)}, bf16[2,4,256,128]{3,2,1,0:T(8,128)(2,1)S(1)}, u32[]{:S(2)}, u32[]{:S(2)}) collective-permute-start(bf16[2,4,256,128]{3,2,1,0:T(8,128)(2,1)S(1)} %get-tuple-element.46), channel_id=1, source_target_pairs={{0,8},{8,0},{16,24},{24,16},{1,9},{9,1},{17,25},{25,17},{2,10},{10... | collective-permute-start | bytes 1572872 | tf_op jit(solution)/shard_map/ppermute | solution.py:265
  33.2 10.0 %collective-permute-start.14 = (bf16[1,4,256,128]{3,2,1,0:T(8,128)(2,1)S(1)}, bf16[1,4,256,128]{3,2,1,0:T(8,128)(2,1)S(1)}, u32[]{:S(2)}, u32[]{:S(2)}) collective-permute-start(bf16[1,4,256,128]{3,2,1,0:T(8,128)(2,1)S(1)} %get-tuple-element.45), channel_id=1, source_target_pairs={{0,16},{8,24},{16,0},{24,8},{1,17},{9,25},{17,1},{25,9},{2,18},{10... | collective-permute-start | bytes 786440 | tf_op jit(solution)/shard_map/ppermute | solution.py:265
  36.1 12.8 %collective-permute-start.12 = (bf16[1,4,256,128]{3,2,1,0:T(8,128)(2,1)S(1)}, bf16[1,4,256,128]{3,2,1,0:T(8,128)(2,1)S(1)}, u32[]{:S(2)}, u32[]{:S(2)}) collective-permute-start(bf16[1,4,256,128]{3,2,1,0:T(8,128)(2,1)S(1)} %get-tuple-element.31.after_ref), channel_id=1, source_target_pairs={{0,16},{8,24},{16,0},{24,8},{1,17},{9,25},{17,1},{25,9},{2,18},{10... | collective-permute-start | bytes 786440 | tf_op jit(solution)/shard_map/ppermute | solution.py:265
  43.2 11.2 %collective-permute-start.19 = (bf16[1,4,256,128]{3,2,1,0:T(8,128)(2,1)S(1)}, bf16[1,4,256,128]{3,2,1,0:T(8,128)(2,1)S(1)}, u32[]{:S(2)}, u32[]{:S(2)}) collective-permute-start(bf16[1,4,256,128]{3,2,1,0:T(8,128)(2,1)S(1)} %get-tuple-element.48), channel_id=1, source_target_pairs={{0,16},{8,24},{16,0},{24,8},{1,17},{9,25},{17,1},{25,9},{2,18},{10... | collective-permute-start | bytes 786440 | tf_op jit(solution)/shard_map/ppermute | solution.py:265
  45.2 14.8 %collective-permute-start.17 = (bf16[1,4,256,128]{3,2,1,0:T(8,128)(2,1)S(1)}, bf16[1,4,256,128]{3,2,1,0:T(8,128)(2,1)S(1)}, u32[]{:S(2)}, u32[]{:S(2)}) collective-permute-start(bf16[1,4,256,128]{3,2,1,0:T(8,128)(2,1)S(1)} %get-tuple-element.34.after_ref), channel_id=1, source_target_pairs={{0,16},{8,24},{16,0},{24,8},{1,17},{9,25},{17,1},{25,9},{2,18},{10... | collective-permute-start | bytes 786440 | tf_op jit(solution)/shard_map/ppermute | solution.py:265
  48.8 16.9 %collective-permute-start.5 = (bf16[1,4,256,128]{3,2,1,0:T(8,128)(2,1)S(1)}, bf16[1,4,256,128]{3,2,1,0:T(8,128)(2,1)S(1)}, u32[]{:S(2)}, u32[]{:S(2)}) collective-permute-start(bf16[1,4,256,128]{3,2,1,0:T(8,128)(2,1)S(1)} %get-tuple-element.40), channel_id=1, source_target_pairs={{0,16},{8,24},{16,0},{24,8},{1,17},{9,25},{17,1},{25,9},{2,18},{10... | collective-permute-start | bytes 786440 | tf_op jit(solution)/shard_map/ppermute | solution.py:265
  51.1 20.2 %collective-permute-start.7 = (bf16[1,4,256,128]{3,2,1,0:T(8,128)(2,1)S(1)}, bf16[1,4,256,128]{3,2,1,0:T(8,128)(2,1)S(1)}, u32[]{:S(2)}, u32[]{:S(2)}) collective-permute-start(bf16[1,4,256,128]{3,2,1,0:T(8,128)(2,1)S(1)} %get-tuple-element.41), channel_id=1, source_target_pairs={{0,16},{8,24},{16,0},{24,8},{1,17},{9,25},{17,1},{25,9},{2,18},{10... | collective-permute-start | bytes 786440 | tf_op jit(solution)/shard_map/ppermute | solution.py:265
  54.4 22.5 %collective-permute-start.9 = (bf16[1,4,256,128]{3,2,1,0:T(8,128)(2,1)S(1)}, bf16[1,4,256,128]{3,2,1,0:T(8,128)(2,1)S(1)}, u32[]{:S(2)}, u32[]{:S(2)}) collective-permute-start(bf16[1,4,256,128]{3,2,1,0:T(8,128)(2,1)S(1)} %get-tuple-element.42), channel_id=1, source_target_pairs={{0,16},{8,24},{16,0},{24,8},{1,17},{9,25},{17,1},{25,9},{2,18},{10... | collective-permute-start | bytes 786440 | tf_op jit(solution)/shard_map/ppermute | solution.py:265
  60.1 31.7 %collective-permute-start.13 = (bf16[1,4,256,128]{3,2,1,0:T(8,128)(2,1)S(1)}, bf16[1,4,256,128]{3,2,1,0:T(8,128)(2,1)S(1)}, u32[]{:S(2)}, u32[]{:S(2)}) collective-permute-start(bf16[1,4,256,128]{3,2,1,0:T(8,128)(2,1)S(1)} %add_blocks.18), channel_id=1, source_target_pairs={{0,4},{1,5},{2,6},{3,7},{4,0},{5,1},{6,2},{7,3},{8,12},{9,13},{10,... | collective-permute-start | bytes 786440 | tf_op jit(solution)/shard_map/ppermute | solution.py:265
  63.2 35.1 %collective-permute-start.15 = (bf16[1,4,256,128]{3,2,1,0:T(8,128)(2,1)S(1)}, bf16[1,4,256,128]{3,2,1,0:T(8,128)(2,1)S(1)}, u32[]{:S(2)}, u32[]{:S(2)}) collective-permute-start(bf16[1,4,256,128]{3,2,1,0:T(8,128)(2,1)S(1)} %add_blocks.19), channel_id=1, source_target_pairs={{0,5},{1,4},{2,7},{3,6},{4,1},{5,0},{6,3},{7,2},{8,13},{9,12},{10,... | collective-permute-start | bytes 786440 | tf_op jit(solution)/shard_map/ppermute | solution.py:265
  65.7 33.4 %collective-permute-start.4 = (bf16[1,4,256,128]{3,2,1,0:T(8,128)(2,1)S(1)}, bf16[1,4,256,128]{3,2,1,0:T(8,128)(2,1)S(1)}, u32[]{:S(2)}, u32[]{:S(2)}) collective-permute-start(bf16[1,4,256,128]{3,2,1,0:T(8,128)(2,1)S(1)} %get-tuple-element.39), channel_id=1, source_target_pairs={{0,16},{8,24},{16,0},{24,8},{1,17},{9,25},{17,1},{25,9},{2,18},{10... | collective-permute-start | bytes 786440 | tf_op jit(solution)/shard_map/ppermute | solution.py:265
  68.7 32.3 %copy-start.5 = (s32[8,8,4]{1,2,0:T(4,128)S(1)}, s32[8,8,4]{1,2,0:T(4,128)}, u32[]{:S(2)}) copy-start(s32[8,8,4]{1,2,0:T(4,128)} %param.9) | copy-start | bytes 3076
  71.3 30.1 %collective-permute-start.18 = (bf16[1,4,256,128]{3,2,1,0:T(8,128)(2,1)}, bf16[1,4,256,128]{3,2,1,0:T(8,128)(2,1)}, u32[]{:S(2)}, u32[]{:S(2)}) collective-permute-start(bf16[1,4,256,128]{3,2,1,0:T(8,128)(2,1)} %add_blocks.20), channel_id=1, source_target_pairs={{0,6},{1,7},{2,4},{3,5},{4,2},{5,3},{6,0},{7,1},{8,14},{9,15},{10,... | collective-permute-start | bytes 786440 | tf_op jit(solution)/shard_map/ppermute | solution.py:265
  76.9 24.5 %collective-permute-start.20 = (bf16[1,4,256,128]{3,2,1,0:T(8,128)(2,1)S(1)}, bf16[1,4,256,128]{3,2,1,0:T(8,128)(2,1)}, u32[]{:S(2)}, u32[]{:S(2)}) collective-permute-start(bf16[1,4,256,128]{3,2,1,0:T(8,128)(2,1)S(1)} %add_blocks.21), channel_id=1, source_target_pairs={{0,7},{1,6},{2,5},{3,4},{4,3},{5,2},{6,1},{7,0},{8,15},{9,14},{10,... | collective-permute-start | bytes 786440 | tf_op jit(solution)/shard_map/ppermute | solution.py:265
  91.8 0.7 copy-start
  92.5 11.2 %collective-permute-start.6 = (bf16[1,4,256,128]{3,2,1,0:T(8,128)(2,1)S(1)}, bf16[1,4,256,128]{3,2,1,0:T(8,128)(2,1)}, u32[]{:S(2)}, u32[]{:S(2)}) collective-permute-start(bf16[1,4,256,128]{3,2,1,0:T(8,128)(2,1)S(1)} %add_blocks.15), channel_id=1, source_target_pairs={{0,1},{1,0},{2,3},{3,2},{4,5},{5,4},{6,7},{7,6},{8,9},{9,8},{10,11... | collective-permute-start | bytes 786440 | tf_op jit(solution)/shard_map/ppermute | solution.py:265
  98.3 0.7 copy-start.2
  99.0 9.0 %collective-permute-start.8 = (bf16[1,4,256,128]{3,2,1,0:T(8,128)(2,1)S(1)}, bf16[1,4,256,128]{3,2,1,0:T(8,128)(2,1)}, u32[]{:S(2)}, u32[]{:S(2)}) collective-permute-start(bf16[1,4,256,128]{3,2,1,0:T(8,128)(2,1)S(1)} %add_blocks.16), channel_id=1, source_target_pairs={{0,2},{1,3},{2,0},{3,1},{4,6},{5,7},{6,4},{7,5},{8,10},{9,11},{10,... | collective-permute-start | bytes 786440 | tf_op jit(solution)/shard_map/ppermute | solution.py:265
  99.1 12.1 %collective-permute-start.10 = (bf16[1,4,256,128]{3,2,1,0:T(8,128)(2,1)S(1)}, bf16[1,4,256,128]{3,2,1,0:T(8,128)(2,1)}, u32[]{:S(2)}, u32[]{:S(2)}) collective-permute-start(bf16[1,4,256,128]{3,2,1,0:T(8,128)(2,1)S(1)} %add_blocks.17), channel_id=1, source_target_pairs={{0,3},{1,2},{2,1},{3,0},{4,7},{5,6},{6,5},{7,4},{8,11},{9,10},{10,... | collective-permute-start | bytes 786440 | tf_op jit(solution)/shard_map/ppermute | solution.py:265
  101.3 9.9 %copy-start.1 = (bf16[1,4,256,128]{3,2,1,0:T(8,128)(2,1)S(1)}, bf16[1,4,256,128]{3,2,1,0:T(8,128)(2,1)}, u32[]{:S(2)}) copy-start(bf16[1,4,256,128]{3,2,1,0:T(8,128)(2,1)} %copy-done) | copy-start | bytes 786436
  101.3 9.9 %copy-start.3 = (bf16[1,4,256,128]{3,2,1,0:T(8,128)(2,1)S(1)}, bf16[1,4,256,128]{3,2,1,0:T(8,128)(2,1)}, u32[]{:S(2)}) copy-start(bf16[1,4,256,128]{3,2,1,0:T(8,128)(2,1)} %copy-done.2) | copy-start | bytes 786436

commit v2 on v1

--- a/solution.py
+++ b/solution.py
@@ -15,8 +15,9 @@
 CODE_BIAS = 128
 BLOCK = 128
 SIDE = 64
-CHUNKS = 8
-EDGES = (0, 2, 4, 8)
+CHUNK_EDGES = (0, 2, 4, 8, 12, 16, 20, 24, 28, 32)
+STAGE_EDGES = (0, 8, 16, 32)
+LATE = 3
 
 
 def fill_coef(scale_ref, cells_ref, codes_ref, write, low_ref, high_ref, weight_ref, table_ref):
@@ -51,20 +52,19 @@
         write(j, table_ref[pl.ds(j * stride, block), :].astype(jnp.bfloat16))
 
 
-def distance_at(position, groups):
+def distances(groups):
     half = groups // 2
-    if isinstance(position, int):
-        return half + position if position < half else groups - 1 - position
-    return jnp.where(position < half, half + position, groups - 1 - position)
+    far, near = list(range(half, groups)), list(range(half - 1, -1, -1))
+    return [far[0], near[0], far[1], near[1]] + far[2:] + near[2:] if half > 2 else far + near
 
 
 def put_products(flip, coef, out_refs):
     product = jnp.dot(flip, coef, preferred_element_type=jnp.float32)
     for n, out_ref in enumerate(out_refs):
-        width = out_ref.shape[2]
-        for c in range(out_ref.shape[1]):
+        width = out_ref.shape[1]
+        for c in range(out_ref.shape[0]):
             part = product[n * width : (n + 1) * width, c * ROWS : (c + 1) * ROWS]
-            out_ref[0, c] = part.astype(jnp.bfloat16)
+            out_ref[c] = part.astype(jnp.bfloat16)
 
 
 def first_kernel(place_ref, scale_ref, cells_ref, codes_ref, *refs, groups):
@@ -100,7 +100,7 @@
             for copy in saves:
                 copy.start()
 
-        owner = place_ref[1] ^ distance_at(step - blocks, groups)
+        owner = place_ref[2 + step - blocks]
         coef = coef_ref[:, pl.ds(pl.multiple_of(owner * span, span), span)]
         put_products(flip_ref[...], coef, out_refs)
 
@@ -115,7 +115,7 @@
     blocks = tokens // BLOCK
     last = blocks - 1
     spec = pl.BlockSpec((pairs, BLOCK), lambda i, *_: (0, jnp.minimum(i, last)))
-    outs = [jax.ShapeDtypeStruct((length, capacity, width, ROWS), jnp.bfloat16) for _ in range(replicas)]
+    outs = [jax.ShapeDtypeStruct((length * capacity, width, ROWS), jnp.bfloat16) for _ in range(replicas)]
     cells_all = TOUCH * ROWS
     return pl.pallas_call(
         functools.partial(first_kernel, groups=groups),
@@ -129,7 +129,7 @@
             ],
             out_specs=[pl.BlockSpec(memory_space=pl.ANY), pl.BlockSpec(memory_space=pl.ANY)]
             + [
-                pl.BlockSpec((1, capacity, width, ROWS), lambda i, *_: (jnp.maximum(i - blocks, 0), 0, 0, 0))
+                pl.BlockSpec((capacity, width, ROWS), lambda i, *_: (jnp.maximum(i - blocks, 0), 0, 0))
                 for _ in outs
             ],
             scratch_shapes=[
@@ -150,7 +150,7 @@
         cost_estimate=pl.CostEstimate(
             flops=2 * tokens * pairs * cells_all * 4, transcendentals=0, bytes_accessed=tokens * cells_all * 4
         ),
-        compiler_params=pltpu.CompilerParams(vmem_limit_bytes=30 << 20),
+        compiler_params=pltpu.CompilerParams(vmem_limit_bytes=26 << 20),
         name="first_products",
     )(place, head_scale, *[pltpu.with_memory_space_constraint(a, pltpu.HBM) for a in [cells, codes] + [grads] * replicas])
 
@@ -159,7 +159,7 @@
     put_products(flip_ref[...], coef_ref[...], out_refs)
 
 
-def rest_products(place, coef, flip, after, replicas, width, capacity, groups, first, stop):
+def rest_products(place, coef, flip, after, replicas, width, capacity, first, stop):
     tokens = coef.shape[0]
     length = stop - first
     return pl.pallas_call(
@@ -168,23 +168,23 @@
             num_scalar_prefetch=1,
             grid=(length,),
             in_specs=[
-                pl.BlockSpec((tokens, capacity * ROWS), lambda i, place: (0, place[1] ^ distance_at(first + i, groups))),
+                pl.BlockSpec((tokens, capacity * ROWS), lambda i, place: (0, place[2 + first + i])),
                 pl.BlockSpec(flip.shape, lambda i, place: (0, 0)),
                 pl.BlockSpec(memory_space=pl.ANY),
             ],
             out_specs=[
-                pl.BlockSpec((1, capacity, width, ROWS), lambda i, place: (i, 0, 0, 0)) for _ in range(replicas)
+                pl.BlockSpec((capacity, width, ROWS), lambda i, place: (i, 0, 0)) for _ in range(replicas)
             ],
         ),
         out_shape=[
-            jax.ShapeDtypeStruct((length, capacity, width, ROWS), jnp.bfloat16) for _ in range(replicas)
+            jax.ShapeDtypeStruct((length * capacity, width, ROWS), jnp.bfloat16) for _ in range(replicas)
         ],
         cost_estimate=pl.CostEstimate(
             flops=2 * tokens * length * capacity * ROWS * width * replicas,
             transcendentals=0,
             bytes_accessed=2 * length * capacity * ROWS * (tokens + replicas * width) + 2 * replicas * width * tokens,
         ),
-        compiler_params=pltpu.CompilerParams(vmem_limit_bytes=24 << 20),
+        compiler_params=pltpu.CompilerParams(vmem_limit_bytes=16 << 20),
         name="rest_products",
     )(place, coef, flip, after)
 
@@ -192,14 +192,13 @@
 def add_kernel(*refs, plan):
     count = len(refs) - len(plan)
     for out_ref, terms in zip(refs[count:], plan):
-        size = out_ref.shape[0]
         total = 0.0
         for n, at in terms:
-            total = total + refs[n][at * size : (at + 1) * size].astype(jnp.float32)
+            total = total + refs[n][at : at + out_ref.shape[0]].astype(jnp.float32)
         out_ref[...] = total.astype(jnp.bfloat16)
 
 
-def add_blocks(sums, size):
+def add_tiles(sums, sizes):
     arrays = []
     plan = []
     for terms in sums:
@@ -211,45 +210,59 @@
                 arrays.append(array)
             row.append((known[0], at))
         plan.append(tuple(row))
-    shape = (size,) + arrays[0].shape[1:]
     spec = pl.BlockSpec(memory_space=pltpu.VMEM)
     return pl.pallas_call(
         functools.partial(add_kernel, plan=tuple(plan)),
         in_specs=[spec for _ in arrays],
         out_specs=[spec for _ in plan],
-        out_shape=[pltpu.VMEM(shape, jnp.bfloat16) for _ in plan],
+        out_shape=[pltpu.VMEM((size,) + arrays[0].shape[1:], jnp.bfloat16) for size in sizes],
         compiler_params=pltpu.CompilerParams(vmem_limit_bytes=4 << 20),
-        name="add_blocks",
+        name="add_tiles",
     )(*[pltpu.with_memory_space_constraint(array, pltpu.VMEM) for array in arrays])
 
 
-def gather_kernel(place_ref, slot_ref, *refs):
-    part_refs, out_ref, sum_ref = refs[:-2], refs[-2], refs[-1]
-    groups = len(part_refs)
-    capacity = part_refs[0].shape[1]
+def gather_kernel(place_ref, slot_ref, *refs, plan, groups, capacity, first, last):
+    refs = list(refs)
+    sum_ref = refs.pop() if last else refs[-1]
+    out_ref = refs.pop()
     owner = place_ref[1]
-    sum_ref[...] = jnp.zeros(sum_ref.shape, jnp.float32)
-    for n, part_ref in enumerate(part_refs):
-        for c in range(capacity):
-            slot = slot_ref[((owner ^ n) * groups + owner) * capacity + c]
-            sum_ref[slot] += part_ref[0, c].astype(jnp.float32)
-    for k in range(OWN):
-        out_ref[pl.ds(k * ROWS, ROWS), :] = sum_ref[k].T.astype(jnp.bfloat16)
-
-
-def gather_tiles(place, slots, parts):
-    width = parts[0].shape[2]
+    if first:
+        sum_ref[...] = jnp.zeros(sum_ref.shape, jnp.float32)
+    else:
+        sum_ref[...] = refs.pop(0)[...]
+    for part_ref, (distance, at) in zip(refs, plan):
+        for n in range(part_ref.shape[0]):
+            slot = slot_ref[((owner ^ distance) * groups + owner) * capacity + at + n]
+            sum_ref[slot] += part_ref[n].astype(jnp.float32)
+    if last:
+        for k in range(OWN):
+            out_ref[pl.ds(k * ROWS, ROWS), :] = sum_ref[k].T.astype(jnp.bfloat16)
+
+
+def gather_tiles(place, slots, parts, groups, capacity, before=None, last=True):
+    width = parts[0][2].shape[1]
     scalars = pl.BlockSpec(memory_space=pltpu.SMEM)
     spec = pl.BlockSpec(memory_space=pltpu.VMEM)
+    arrays = [array for _, _, array in parts]
+    if before is not None:
+        arrays.insert(0, before)
+    total = pltpu.VMEM((OWN, width, ROWS), jnp.float32)
     return pl.pallas_call(
-        gather_kernel,
-        in_specs=[scalars, scalars] + [spec for _ in parts],
+        functools.partial(
+            gather_kernel,
+            plan=tuple((distance, at) for distance, at, _ in parts),
+            groups=groups,
+            capacity=capacity,
+            first=before is None,
+            last=last,
+        ),
+        in_specs=[scalars, scalars] + [spec for _ in arrays],
         out_specs=spec,
-        scratch_shapes=[pltpu.VMEM((OWN, width, ROWS), jnp.float32)],
-        out_shape=jax.ShapeDtypeStruct((OWN * ROWS, width), jnp.bfloat16),
+        scratch_shapes=[total] if last else [],
+        out_shape=jax.ShapeDtypeStruct((OWN * ROWS, width), jnp.bfloat16) if last else total,
         compiler_params=pltpu.CompilerParams(vmem_limit_bytes=6 << 20),
         name="gather_tiles",
-    )(place, slots, *[pltpu.with_memory_space_constraint(part, pltpu.VMEM) for part in parts])
+    )(place, slots, *[pltpu.with_memory_space_constraint(array, pltpu.VMEM) for array in arrays])
 
 
 def body(out_grad, pair_cells, weight_codes, head_scale, touch_slots, *, replicas):
@@ -258,18 +271,20 @@
     groups = touch_slots.shape[0]
     capacity = touch_slots.shape[2]
     pairs = pair_cells.shape[1] * pair_cells.shape[2]
-    place = jnp.stack([lax.axis_index("dp"), lax.axis_index("table")]).astype(jnp.int32)
+    order = distances(groups)
+    owner = lax.axis_index("table")
+    place = jnp.stack([lax.axis_index("dp"), owner] + [owner ^ n for n in order]).astype(jnp.int32)
     by_pair = lambda array: array.transpose(1, 2, 0).reshape(pairs, tokens)
 
     def swap(array, axis, bit):
         return lax.ppermute(array, axis, [(i, i ^ bit) for i in range(lax.axis_size(axis))])
 
-    chunks = min(CHUNKS, groups)
-    size = groups // chunks
-    edges = sorted({max(edge and 1, edge * chunks // CHUNKS) for edge in EDGES})
-    pieces = [{m: [] for m in range(0, replicas, 2)} for _ in range(chunks)]
+    tiles = groups * capacity
+    chunks = [(a * tiles // TOUCH, b * tiles // TOUCH) for a, b in zip(CHUNK_EDGES, CHUNK_EDGES[1:])]
+    stages = [(a * tiles // TOUCH, b * tiles // TOUCH) for a, b in zip(STAGE_EDGES, STAGE_EDGES[1:])]
+    pieces = [{m: [] for m in range(0, replicas, 2)} for _ in chunks]
     sent = None
-    for stage, (first, stop) in enumerate(zip(edges, edges[1:])):
+    for stage, (first, stop) in enumerate(stages):
         if stage == 0:
             coef, flip, *outs = first_products(
                 place,
@@ -281,34 +296,44 @@
                 width,
                 capacity,
                 groups,
-                stop * size,
+                stop // capacity,
             )
         else:
-            outs = rest_products(place, coef, flip, sent, replicas, width, capacity, groups, first * size, stop * size)
+            outs = rest_products(
+                place, coef, flip, sent, replicas, width, capacity, first // capacity, stop // capacity
+            )
+        here = [n for n, (a, b) in enumerate(chunks) if first <= a < stop]
+        sizes = [chunks[n][1] - chunks[n][0] for n in here]
         for m in sorted(range(replicas), reverse=True):
             array = swap(outs[m], "dp", 1) if m & 1 else outs[m]
-            for n in range(first, stop):
-                pieces[n][m & ~1].append((array, n - first))
-        some = pieces[first:stop]
+            for n in here:
+                pieces[n][m & ~1].append((array, chunks[n][0] - first))
         sent = outs[0]
         bit = 2
         while bit < replicas:
-            masks = [m for m in sorted(some[0], reverse=True) if m & bit]
-            sums = add_blocks([piece.pop(m) for piece in some for m in masks], size)
+            masks = [m for m in sorted(pieces[here[0]], reverse=True) if m & bit]
+            sums = add_tiles(
+                [pieces[n].pop(m) for n in here for m in masks], [size for size in sizes for _ in masks]
+            )
             sent = sums[0] if bit == 2 else sent
             sums = iter(sums)
-            for n, piece in enumerate(some, first):
+            for n in here:
                 for m in masks:
-                    piece[m ^ bit].append((swap(next(sums), "dp", bit), 0))
+                    pieces[n][m ^ bit].append((swap(next(sums), "dp", bit), 0))
             bit *= 2
-    parts = {}
-    for chunk, piece in enumerate(pieces):
-        (mine,) = add_blocks([piece[0]], size)
-        for i in range(size):
-            distance = distance_at(chunk * size + i, groups)
-            part = mine if size == 1 else mine[i : i + 1]
-            parts[distance] = swap(part, "table", distance) if distance else part
-    return gather_tiles(place, touch_slots.reshape(-1), [parts[n] for n in range(groups)])
+    parts = []
+    for (a, b), piece in zip(chunks, pieces):
+        (mine,) = add_tiles([piece[0]], [b - a])
+        for start in range(a, b, min(capacity, b - a)):
+            stop = min(start + capacity, b)
+            distance = order[start // capacity]
+            part = mine if stop - start == b - a else mine[start - a : stop - a]
+            part = swap(part, "table", distance) if distance else part
+            parts.append((distance, start % capacity, part))
+    slots = touch_slots.reshape(-1)
+    late = len(parts) - LATE
+    total = gather_tiles(place, slots, parts[:late], groups, capacity, last=False)
+    return gather_tiles(place, slots, parts[late:], groups, capacity, before=total)
 
 
 def solution(mesh):

time: 116 us -> 117 us (level)
  the two profiles are of different devices: /device:TPU:0 before, /device:TPU:19 now
where the time goes in v2:
time: 117 us; the launch traced here: 116 us
  waiting for transfers between devices  64.9 us (55%)
  Pallas kernels  33.4 us (29%)
  starting transfers between devices  14.3 us (12%)
  local copies, waits for them, and re-layouts  3.69 us (3%)
    ppermute x23, waiting for transfers between devices, swap(): lax.ppermute(array, axis, [(i, i ^ bit) for i in range(lax.axis_size(axis...  64.9 us
    pallas_call x1, Pallas kernels, first_products(): pl.pallas_call(functools.partial(first_kernel, groups=groups), grid_spec=...  17.8 us
    ppermute x23, starting transfers between devices, swap(): lax.ppermute(array, axis, [(i, i ^ bit) for i in range(lax.axis_size(axis...  14.3 us
    pallas_call x2, Pallas kernels, rest_products(): pl.pallas_call(rest_kernel, grid_spec=pltpu.PrefetchScalarGridSpec(num_sc...  9.24 us
    pallas_call x2, Pallas kernels, gather_tiles(): pl.pallas_call(functools.partial(gather_kernel, plan=tuple(((distance, at...  3.69 us
    unnamed x7, local copies, waits for them, and re-layouts  2.75 us
    pallas_call x12, Pallas kernels, add_tiles(): pl.pallas_call(functools.partial(add_kernel, plan=tuple(plan)), in_specs=...  2.68 us
  transfers between devices with their start and end apart: 23, of which 16 were waited for; matrix products, arithmetic and copies ran while one was open for 2% of the time, Pallas kernels for 3%

profile of v2, /device:TPU:19, one launch (start us, length us, event | category | flops | bytes accessed | tf_op | source)
XLA Modules:
  0.0 116.4 jit_solution(3673264176071378965)
XLA Ops:
  0.1 0.7 copy-done.2
  0.7 17.8 %first_products.1 = (bf16[1024,4096]{1,0:T(8,128)(2,1)S(1)}, bf16[1024,1024]{1,0:T(8,128)(2,1)S(1)}, bf16[8,256,128]{2,1,0:T(8,128)(2,1)S(1)}, bf16[8,256,128]{2...) custom-call(s32[10]{0:T(128)S(1)} %stack.40.place_ref, f32[8]{0:T(128)S(1)} %copy-done.2, ...), custom_call_target="tpu_custom_call" | custom-call | flops 8589934592 | bytes 16777216 | tf_op jit(solution)/shard_map/first_products/pallas_call | solution.py:120
  18.6 0.7 collective-permute-start.1
  19.3 1.5 %collective-permute-done.1.refs_0_ = bf16[8,256,128]{2,1,0:T(8,128)(2,1)S(1)} collective-permute-done((bf16[8,256,128]{2,1,0:T(8,128)(2,1)S(1)}, bf16[8,256,128]{2,1,0:T(8,128)(2,1)S(1)}, u32[]{:S(2)}, u32[]{:S(2)}) %collective-permute-start.1) | collective-permute-done | bytes 524320 | tf_op jit(solution)/shard_map/ppermute | solution.py:280
  21.0 3.3 %rest_products.2 = (bf16[8,256,128]{2,1,0:T(8,128)(2,1)S(1)}, bf16[8,256,128]{2,1,0:T(8,128)(2,1)S(1)}, bf16[8,256,128]{2,1,0:T(8,128)(2,1)S(1)}, bf16[8,256,128]{2,1,0:T(8,128)(2,1)S(1)}) custom-call(s32[10]{0:T(128)S(1)} %stack.40.place_ref, bf16[1024,4096]{1,0:T(8,128)(2,1)S(1)} %get-tuple-element.35.coef_ref, ...), custom_call_target="tpu_custom_call" | custom-call | flops 2147483648 | bytes 6291456 | tf_op jit(solution)/shard_map/rest_products/pallas_call | solution.py:165
  24.3 0.4 collective-permute-start.9
  24.7 1.5 %collective-permute-done.9.refs_0_ = bf16[8,256,128]{2,1,0:T(8,128)(2,1)S(1)} collective-permute-done((bf16[8,256,128]{2,1,0:T(8,128)(2,1)S(1)}, bf16[8,256,128]{2,1,0:T(8,128)(2,1)S(1)}, u32[]{:S(2)}, u32[]{:S(2)}) %collective-permute-start.9) | collective-permute-done | bytes 524320 | tf_op jit(solution)/shard_map/ppermute | solution.py:280
  26.4 6.0 %rest_products.3 = (bf16[16,256,128]{2,1,0:T(8,128)(2,1)S(1)}, bf16[16,256,128]{2,1,0:T(8,128)(2,1)S(1)}, bf16[16,256,128]{2,1,0:T(8,128)(2,1)S(1)}, bf16[16,256,128]{2,1,0:T(8,128)(2,1)S(1)}) custom-call(s32[10]{0:T(128)S(1)} %stack.40.place_ref, bf16[1024,4096]{1,0:T(8,128)(2,1)S(1)} %get-tuple-element.35.coef_ref, ...), custom_call_target="tpu_custom_call" | custom-call | flops 4294967296 | bytes 10485760 | tf_op jit(solution)/shard_map/rest_products/pallas_call | solution.py:165
  32.3 0.4 collective-permute-start.15
  32.9 0.4 collective-permute-start
  33.3 0.1 collective-permute-start.8
  33.4 0.2 collective-permute-start.2
  33.7 3.6 %collective-permute-done.refs_0_ = bf16[8,256,128]{2,1,0:T(8,128)(2,1)S(1)} collective-permute-done((bf16[8,256,128]{2,1,0:T(8,128)(2,1)S(1)}, bf16[8,256,128]{2,1,0:T(8,128)(2,1)S(1)}, u32[]{:S(2)}, u32[]{:S(2)}) %collective-permute-start) | collective-permute-done | bytes 524320 | tf_op jit(solution)/shard_map/ppermute | solution.py:280
  37.3 0.2 collective-permute-start.4
  37.6 0.5 collective-permute-done.2.refs_2_
  38.1 0.7 collective-permute-start.6
  38.8 3.2 %collective-permute-done.4.refs_2_ = bf16[2,256,128]{2,1,0:T(8,128)(2,1)S(1)} collective-permute-done((bf16[2,256,128]{2,1,0:T(8,128)(2,1)S(1)}, bf16[2,256,128]{2,1,0:T(8,128)(2,1)S(1)}, u32[]{:S(2)}, u32[]{:S(2)}) %collective-permute-start.4) | collective-permute-done | bytes 131104 | tf_op jit(solution)/shard_map/ppermute | solution.py:280
  42.0 0.2 collective-permute-start.10
  42.3 1.2 %collective-permute-start.12 = (bf16[4,256,128]{2,1,0:T(8,128)(2,1)S(1)}, bf16[4,256,128]{2,1,0:T(8,128)(2,1)S(1)}, u32[]{:S(2)}, u32[]{:S(2)}) collective-permute-start(bf16[4,256,128]{2,1,0:T(8,128)(2,1)S(1)} %get-tuple-element.42), channel_id=1, source_target_pairs={{0,16},{8,24},{16,0},{24,8},{1,17},{9,25},{17,1},{25,9},{2,18},{10... | collective-permute-start | bytes 786440 | tf_op jit(solution)/shard_map/ppermute | solution.py:280
  43.5 0.2 add_tiles.19
  43.7 3.9 %collective-permute-done.6.refs_2_ = bf16[4,256,128]{2,1,0:T(8,128)(2,1)S(1)} collective-permute-done((bf16[4,256,128]{2,1,0:T(8,128)(2,1)S(1)}, bf16[4,256,128]{2,1,0:T(8,128)(2,1)S(1)}, u32[]{:S(2)}, u32[]{:S(2)}) %collective-permute-start.6) | collective-permute-done | bytes 262176 | tf_op jit(solution)/shard_map/ppermute | solution.py:280
  47.6 0.2 collective-permute-start.16
  47.9 1.2 %collective-permute-start.18 = (bf16[4,256,128]{2,1,0:T(8,128)(2,1)S(1)}, bf16[4,256,128]{2,1,0:T(8,128)(2,1)S(1)}, u32[]{:S(2)}, u32[]{:S(2)}) collective-permute-start(bf16[4,256,128]{2,1,0:T(8,128)(2,1)S(1)} %get-tuple-element.48), channel_id=1, source_target_pairs={{0,16},{8,24},{16,0},{24,8},{1,17},{9,25},{17,1},{25,9},{2,18},{10... | collective-permute-start | bytes 786440 | tf_op jit(solution)/shard_map/ppermute | solution.py:280
  49.1 4.1 %collective-permute-done.10.refs_2_ = bf16[4,256,128]{2,1,0:T(8,128)(2,1)S(1)} collective-permute-done((bf16[4,256,128]{2,1,0:T(8,128)(2,1)S(1)}, bf16[4,256,128]{2,1,0:T(8,128)(2,1)S(1)}, u32[]{:S(2)}, u32[]{:S(2)}) %collective-permute-start.10) | collective-permute-done | bytes 262176 | tf_op jit(solution)/shard_map/ppermute | solution.py:280
  53.2 0.2 collective-permute-start.20
  53.6 5.3 %collective-permute-done.12.refs_2_ = bf16[4,256,128]{2,1,0:T(8,128)(2,1)S(1)} collective-permute-done((bf16[4,256,128]{2,1,0:T(8,128)(2,1)S(1)}, bf16[4,256,128]{2,1,0:T(8,128)(2,1)S(1)}, u32[]{:S(2)}, u32[]{:S(2)}) %collective-permute-start.12) | collective-permute-done | bytes 262176 | tf_op jit(solution)/shard_map/ppermute | solution.py:280
  58.9 2.2 %collective-permute-start.7 = (bf16[4,256,128]{2,1,0:T(8,128)(2,1)S(1)}, bf16[4,256,128]{2,1,0:T(8,128)(2,1)S(1)}, u32[]{:S(2)}, u32[]{:S(2)}) collective-permute-start(bf16[4,256,128]{2,1,0:T(8,128)(2,1)S(1)} %add_tiles.15), channel_id=1, source_target_pairs={{0,3},{1,2},{2,1},{3,0},{4,7},{5,6},{6,5},{7,4},{8,11},{9,10},{10,... | collective-permute-start | bytes 786440 | tf_op jit(solution)/shard_map/ppermute | solution.py:280
  61.1 0.2 collective-permute-start.22
  61.5 3.0 %collective-permute-done.16.refs_2_ = bf16[4,256,128]{2,1,0:T(8,128)(2,1)S(1)} collective-permute-done((bf16[4,256,128]{2,1,0:T(8,128)(2,1)S(1)}, bf16[4,256,128]{2,1,0:T(8,128)(2,1)S(1)}, u32[]{:S(2)}, u32[]{:S(2)}) %collective-permute-start.16) | collective-permute-done | bytes 262176 | tf_op jit(solution)/shard_map/ppermute | solution.py:280
  64.5 5.6 %collective-permute-done.18.refs_2_ = bf16[4,256,128]{2,1,0:T(8,128)(2,1)S(1)} collective-permute-done((bf16[4,256,128]{2,1,0:T(8,128)(2,1)S(1)}, bf16[4,256,128]{2,1,0:T(8,128)(2,1)S(1)}, u32[]{:S(2)}, u32[]{:S(2)}) %collective-permute-start.18) | collective-permute-done | bytes 262176 | tf_op jit(solution)/shard_map/ppermute | solution.py:280
  70.2 0.8 add_tiles.17
  71.0 0.8 add_tiles.18
  72.0 3.7 %collective-permute-done.20.refs_2_ = bf16[4,256,128]{2,1,0:T(8,128)(2,1)S(1)} collective-permute-done((bf16[4,256,128]{2,1,0:T(8,128)(2,1)S(1)}, bf16[4,256,128]{2,1,0:T(8,128)(2,1)S(1)}, u32[]{:S(2)}, u32[]{:S(2)}) %collective-permute-start.20) | collective-permute-done | bytes 262176 | tf_op jit(solution)/shard_map/ppermute | solution.py:280
  75.7 1.0 collective-permute-start.11
  76.8 1.4 %collective-permute-start.13 = (bf16[4,256,128]{2,1,0:T(8,128)(2,1)}, bf16[4,256,128]{2,1,0:T(8,128)(2,1)}, u32[]{:S(2)}, u32[]{:S(2)}) collective-permute-start(bf16[4,256,128]{2,1,0:T(8,128)(2,1)} %add_tiles.18), channel_id=1, source_target_pairs={{0,2},{1,3},{2,0},{3,1},{4,6},{5,7},{6,4},{7,5},{8,10},{9,11},{10,... | collective-permute-start | bytes 786440 | tf_op jit(solution)/shard_map/ppermute | solution.py:280
  78.2 0.7 copy-done
  78.8 1.3 %collective-permute-start.17 = (bf16[4,256,128]{2,1,0:T(8,128)(2,1)S(1)}, bf16[4,256,128]{2,1,0:T(8,128)(2,1)}, u32[]{:S(2)}, u32[]{:S(2)}) collective-permute-start(bf16[4,256,128]{2,1,0:T(8,128)(2,1)S(1)} %add_tiles.20), channel_id=1, source_target_pairs={{0,6},{1,7},{2,4},{3,5},{4,2},{5,3},{6,0},{7,1},{8,14},{9,15},{10,... | collective-permute-start | bytes 786440 | tf_op jit(solution)/shard_map/ppermute | solution.py:280
  80.1 0.1 collective-permute-start.19
  80.3 1.1 collective-permute-done.22.refs_2_
  81.3 1.2 %collective-permute-start.21 = (bf16[4,256,128]{2,1,0:T(8,128)(2,1)S(1)}, bf16[4,256,128]{2,1,0:T(8,128)(2,1)}, u32[]{:S(2)}, u32[]{:S(2)}) collective-permute-start(bf16[4,256,128]{2,1,0:T(8,128)(2,1)S(1)} %add_tiles.22), channel_id=1, source_target_pairs={{0,1},{1,0},{2,3},{3,2},{4,5},{5,4},{6,7},{7,6},{8,9},{9,8},{10,11... | collective-permute-start | bytes 786440 | tf_op jit(solution)/shard_map/ppermute | solution.py:280
  82.6 1.4 %copy.6 = s32[8,8,4]{2,1,0:T(8,128)} copy(s32[8,8,4]{1,2,0:T(4,128)} %param.9) | data formatting | bytes 2048 | tf_op args[4]
  84.0 0.9 reshape.9.slot_ref
  85.0 2.6 %collective-permute-done.11.refs_3_ = bf16[4,256,128]{2,1,0:T(8,128)(2,1)} collective-permute-done((bf16[4,256,128]{2,1,0:T(8,128)(2,1)}, bf16[4,256,128]{2,1,0:T(8,128)(2,1)}, u32[]{:S(2)}, u32[]{:S(2)}) %collective-permute-start.11) | collective-permute-done | bytes 262176 | tf_op jit(solution)/shard_map/ppermute | solution.py:280
  87.6 0.8 collective-permute-done.13.refs_4_
  88.4 20.2 %collective-permute-done.17.refs_5_ = bf16[4,256,128]{2,1,0:T(8,128)(2,1)} collective-permute-done((bf16[4,256,128]{2,1,0:T(8,128)(2,1)S(1)}, bf16[4,256,128]{2,1,0:T(8,128)(2,1)}, u32[]{:S(2)}, u32[]{:S(2)}) %collective-permute-start.17) | collective-permute-done | bytes 262176 | tf_op jit(solution)/shard_map/ppermute | solution.py:280
  108.6 1.4 %gather_tiles.2.refs_0_ = f32[8,256,128]{2,1,0:T(8,128)S(1)} custom-call(s32[10]{0:T(128)S(1)} %stack.40.place_ref, s32[256]{0:T(256)S(1)} %reshape.9.slot_ref, bf16[2,256,128]{2,1,0:T(8,128)(2,1)S(1)} %collective-permute-done.3.refs_0_, bf16[2,256,128]{2,1,0:T(8,128)(2,1)S(1)} %copy-done.1, bf16[4,256,128]{2,1,0:T(8,128)(2,1)S(1)} %collective-permute-done.7.refs_2_, ...), custom_call_target="tpu_custom_call" | custom-call | tf_op jit(solution)/shard_map/gather_tiles/pallas_call | solution.py:250
  110.0 4.1 %collective-permute-done.19.refs_1_ = bf16[4,256,128]{2,1,0:T(8,128)(2,1)} collective-permute-done((bf16[4,256,128]{2,1,0:T(8,128)(2,1)S(1)}, bf16[4,256,128]{2,1,0:T(8,128)(2,1)}, u32[]{:S(2)}, u32[]{:S(2)}) %collective-permute-start.19) | collective-permute-done | bytes 262176 | tf_op jit(solution)/shard_map/ppermute | solution.py:280
  114.1 2.3 %gather_tiles.3 = bf16[1024,256]{1,0:T(8,128)(2,1)} custom-call(s32[10]{0:T(128)S(1)} %stack.40.place_ref, s32[256]{0:T(256)S(1)} %reshape.9.slot_ref, f32[8,256,128]{2,1,0:T(8,128)S(1)} %gather_tiles.2.refs_0_, bf16[4,256,128]{2,1,0:T(8,128)(2,1)} %collective-permute-done.19.refs_1_, bf16[4,256,128]{2,1,0:T(8,128)(2,1)} %collective-permute-done.21.refs_2_, ...), custom_call_target="tpu_custom_call" | custom-call | tf_op jit(solution)/shard_map/gather_tiles/pallas_call | solution.py:250
  (24 shorter events, 1.2 us)
Async XLA Ops:
  0.1 0.7 copy-start.2
  18.6 2.3 %collective-permute-start.1 = (bf16[8,256,128]{2,1,0:T(8,128)(2,1)S(1)}, bf16[8,256,128]{2,1,0:T(8,128)(2,1)S(1)}, u32[]{:S(2)}, u32[]{:S(2)}) collective-permute-start(bf16[8,256,128]{2,1,0:T(8,128)(2,1)S(1)} %get-tuple-element.30), channel_id=1, source_target_pairs={{0,8},{8,0},{16,24},{24,16},{1,9},{9,1},{17,25},{25,17},{2,10},{10... | collective-permute-start | bytes 1572872 | tf_op jit(solution)/shard_map/ppermute | solution.py:280
  24.3 2.0 %collective-permute-start.9 = (bf16[8,256,128]{2,1,0:T(8,128)(2,1)S(1)}, bf16[8,256,128]{2,1,0:T(8,128)(2,1)S(1)}, u32[]{:S(2)}, u32[]{:S(2)}) collective-permute-start(bf16[8,256,128]{2,1,0:T(8,128)(2,1)S(1)} %get-tuple-element.39), channel_id=1, source_target_pairs={{0,8},{8,0},{16,24},{24,16},{1,9},{9,1},{17,25},{25,17},{2,10},{10... | collective-permute-start | bytes 1572872 | tf_op jit(solution)/shard_map/ppermute | solution.py:280
  32.3 9.9 %collective-permute-start.15 = (bf16[16,256,128]{2,1,0:T(8,128)(2,1)S(1)}, bf16[16,256,128]{2,1,0:T(8,128)(2,1)S(1)}, u32[]{:S(2)}, u32[]{:S(2)}) collective-permute-start(bf16[16,256,128]{2,1,0:T(8,128)(2,1)S(1)} %get-tuple-element.45), channel_id=1, source_target_pairs={{0,8},{8,0},{16,24},{24,16},{1,9},{9,1},{17,25},{25,17},{2,10},{10... | collective-permute-start | bytes 3145736 | tf_op jit(solution)/shard_map/ppermute | solution.py:280
  32.8 28.3 %collective-permute-start.14 = (bf16[16,256,128]{2,1,0:T(8,128)(2,1)S(1)}, bf16[16,256,128]{2,1,0:T(8,128)(2,1)S(1)}, u32[]{:S(2)}, u32[]{:S(2)}) collective-permute-start(bf16[16,256,128]{2,1,0:T(8,128)(2,1)S(1)} %get-tuple-element.43), channel_id=1, source_target_pairs={{0,8},{8,0},{16,24},{24,16},{1,9},{9,1},{17,25},{25,17},{2,10},{10... | collective-permute-start | bytes 3145736 | tf_op jit(solution)/shard_map/ppermute | solution.py:280
  32.9 4.4 %collective-permute-start = (bf16[8,256,128]{2,1,0:T(8,128)(2,1)S(1)}, bf16[8,256,128]{2,1,0:T(8,128)(2,1)S(1)}, u32[]{:S(2)}, u32[]{:S(2)}) collective-permute-start(bf16[8,256,128]{2,1,0:T(8,128)(2,1)S(1)} %get-tuple-element.28), channel_id=1, source_target_pairs={{0,8},{8,0},{16,24},{24,16},{1,9},{9,1},{17,25},{25,17},{2,10},{10... | collective-permute-start | bytes 1572872 | tf_op jit(solution)/shard_map/ppermute | solution.py:280
  33.3 14.6 %collective-permute-start.8 = (bf16[8,256,128]{2,1,0:T(8,128)(2,1)S(1)}, bf16[8,256,128]{2,1,0:T(8,128)(2,1)S(1)}, u32[]{:S(2)}, u32[]{:S(2)}) collective-permute-start(bf16[8,256,128]{2,1,0:T(8,128)(2,1)S(1)} %get-tuple-element.37), channel_id=1, source_target_pairs={{0,8},{8,0},{16,24},{24,16},{1,9},{9,1},{17,25},{25,17},{2,10},{10... | collective-permute-start | bytes 1572872 | tf_op jit(solution)/shard_map/ppermute | solution.py:280
  33.4 4.7 %collective-permute-start.2 = (bf16[2,256,128]{2,1,0:T(8,128)(2,1)S(1)}, bf16[2,256,128]{2,1,0:T(8,128)(2,1)S(1)}, u32[]{:S(2)}, u32[]{:S(2)}) collective-permute-start(bf16[2,256,128]{2,1,0:T(8,128)(2,1)S(1)} %get-tuple-element.32.after_ref), channel_id=1, source_target_pairs={{0,16},{8,24},{16,0},{24,8},{1,17},{9,25},{17,1},{25,9},{2,18},{10... | collective-permute-start | bytes 393224 | tf_op jit(solution)/shard_map/ppermute | solution.py:280
  37.3 4.7 %collective-permute-start.4 = (bf16[2,256,128]{2,1,0:T(8,128)(2,1)S(1)}, bf16[2,256,128]{2,1,0:T(8,128)(2,1)S(1)}, u32[]{:S(2)}, u32[]{:S(2)}) collective-permute-start(bf16[2,256,128]{2,1,0:T(8,128)(2,1)S(1)} %get-tuple-element.33), channel_id=1, source_target_pairs={{0,16},{8,24},{16,0},{24,8},{1,17},{9,25},{17,1},{25,9},{2,18},{10... | collective-permute-start | bytes 393224 | tf_op jit(solution)/shard_map/ppermute | solution.py:280
  38.1 9.5 %collective-permute-start.6 = (bf16[4,256,128]{2,1,0:T(8,128)(2,1)S(1)}, bf16[4,256,128]{2,1,0:T(8,128)(2,1)S(1)}, u32[]{:S(2)}, u32[]{:S(2)}) collective-permute-start(bf16[4,256,128]{2,1,0:T(8,128)(2,1)S(1)} %get-tuple-element.34), channel_id=1, source_target_pairs={{0,16},{8,24},{16,0},{24,8},{1,17},{9,25},{17,1},{25,9},{2,18},{10... | collective-permute-start | bytes 786440 | tf_op jit(solution)/shard_map/ppermute | solution.py:280
  42.0 11.2 %collective-permute-start.10 = (bf16[4,256,128]{2,1,0:T(8,128)(2,1)S(1)}, bf16[4,256,128]{2,1,0:T(8,128)(2,1)S(1)}, u32[]{:S(2)}, u32[]{:S(2)}) collective-permute-start(bf16[4,256,128]{2,1,0:T(8,128)(2,1)S(1)} %get-tuple-element.41.after_ref), channel_id=1, source_target_pairs={{0,16},{8,24},{16,0},{24,8},{1,17},{9,25},{17,1},{25,9},{2,18},{10... | collective-permute-start | bytes 786440 | tf_op jit(solution)/shard_map/ppermute | solution.py:280
  42.3 16.6 %collective-permute-start.12 = (bf16[4,256,128]{2,1,0:T(8,128)(2,1)S(1)}, bf16[4,256,128]{2,1,0:T(8,128)(2,1)S(1)}, u32[]{:S(2)}, u32[]{:S(2)}) collective-permute-start(bf16[4,256,128]{2,1,0:T(8,128)(2,1)S(1)} %get-tuple-element.42), channel_id=1, source_target_pairs={{0,16},{8,24},{16,0},{24,8},{1,17},{9,25},{17,1},{25,9},{2,18},{10... | collective-permute-start | bytes 786440 | tf_op jit(solution)/shard_map/ppermute | solution.py:280
  47.6 16.9 %collective-permute-start.16 = (bf16[4,256,128]{2,1,0:T(8,128)(2,1)S(1)}, bf16[4,256,128]{2,1,0:T(8,128)(2,1)S(1)}, u32[]{:S(2)}, u32[]{:S(2)}) collective-permute-start(bf16[4,256,128]{2,1,0:T(8,128)(2,1)S(1)} %get-tuple-element.47), channel_id=1, source_target_pairs={{0,16},{8,24},{16,0},{24,8},{1,17},{9,25},{17,1},{25,9},{2,18},{10... | collective-permute-start | bytes 786440 | tf_op jit(solution)/shard_map/ppermute | solution.py:280
  47.9 22.2 %collective-permute-start.18 = (bf16[4,256,128]{2,1,0:T(8,128)(2,1)S(1)}, bf16[4,256,128]{2,1,0:T(8,128)(2,1)S(1)}, u32[]{:S(2)}, u32[]{:S(2)}) collective-permute-start(bf16[4,256,128]{2,1,0:T(8,128)(2,1)S(1)} %get-tuple-element.48), channel_id=1, source_target_pairs={{0,16},{8,24},{16,0},{24,8},{1,17},{9,25},{17,1},{25,9},{2,18},{10... | collective-permute-start | bytes 786440 | tf_op jit(solution)/shard_map/ppermute | solution.py:280
  53.2 22.5 %collective-permute-start.20 = (bf16[4,256,128]{2,1,0:T(8,128)(2,1)S(1)}, bf16[4,256,128]{2,1,0:T(8,128)(2,1)S(1)}, u32[]{:S(2)}, u32[]{:S(2)}) collective-permute-start(bf16[4,256,128]{2,1,0:T(8,128)(2,1)S(1)} %get-tuple-element.49), channel_id=1, source_target_pairs={{0,16},{8,24},{16,0},{24,8},{1,17},{9,25},{17,1},{25,9},{2,18},{10... | collective-permute-start | bytes 786440 | tf_op jit(solution)/shard_map/ppermute | solution.py:280
  58.9 21.3 %collective-permute-start.7 = (bf16[4,256,128]{2,1,0:T(8,128)(2,1)S(1)}, bf16[4,256,128]{2,1,0:T(8,128)(2,1)S(1)}, u32[]{:S(2)}, u32[]{:S(2)}) collective-permute-start(bf16[4,256,128]{2,1,0:T(8,128)(2,1)S(1)} %add_tiles.15), channel_id=1, source_target_pairs={{0,3},{1,2},{2,1},{3,0},{4,7},{5,6},{6,5},{7,4},{8,11},{9,10},{10,... | collective-permute-start | bytes 786440 | tf_op jit(solution)/shard_map/ppermute | solution.py:280
  61.1 20.2 %collective-permute-start.22 = (bf16[4,256,128]{2,1,0:T(8,128)(2,1)S(1)}, bf16[4,256,128]{2,1,0:T(8,128)(2,1)S(1)}, u32[]{:S(2)}, u32[]{:S(2)}) collective-permute-start(bf16[4,256,128]{2,1,0:T(8,128)(2,1)S(1)} %get-tuple-element.50), channel_id=1, source_target_pairs={{0,16},{8,24},{16,0},{24,8},{1,17},{9,25},{17,1},{25,9},{2,18},{10... | collective-permute-start | bytes 786440 | tf_op jit(solution)/shard_map/ppermute | solution.py:280
  64.5 12.3 %collective-permute-start.3 = (bf16[2,256,128]{2,1,0:T(8,128)(2,1)S(1)}, bf16[2,256,128]{2,1,0:T(8,128)(2,1)S(1)}, u32[]{:S(2)}, u32[]{:S(2)}) collective-permute-start(bf16[2,256,128]{2,1,0:T(8,128)(2,1)S(1)} %add_tiles.13), channel_id=1, source_target_pairs={{0,4},{1,5},{2,6},{3,7},{4,0},{5,1},{6,2},{7,3},{8,12},{9,13},{10,... | collective-permute-start | bytes 393224 | tf_op jit(solution)/shard_map/ppermute | solution.py:280
  70.1 8.1 %collective-permute-start.5 = (bf16[2,256,128]{2,1,0:T(8,128)(2,1)S(1)}, bf16[2,256,128]{2,1,0:T(8,128)(2,1)S(1)}, u32[]{:S(2)}, u32[]{:S(2)}) collective-permute-start(bf16[2,256,128]{2,1,0:T(8,128)(2,1)S(1)} %add_tiles.14), channel_id=1, source_target_pairs={{0,4},{1,5},{2,6},{3,7},{4,0},{5,1},{6,2},{7,3},{8,12},{9,13},{10,... | collective-permute-start | bytes 393224 | tf_op jit(solution)/shard_map/ppermute | solution.py:280
  75.7 11.9 %collective-permute-start.11 = (bf16[4,256,128]{2,1,0:T(8,128)(2,1)}, bf16[4,256,128]{2,1,0:T(8,128)(2,1)}, u32[]{:S(2)}, u32[]{:S(2)}) collective-permute-start(bf16[4,256,128]{2,1,0:T(8,128)(2,1)} %add_tiles.17), channel_id=1, source_target_pairs={{0,5},{1,4},{2,7},{3,6},{4,1},{5,0},{6,3},{7,2},{8,13},{9,12},{10,... | collective-permute-start | bytes 786440 | tf_op jit(solution)/shard_map/ppermute | solution.py:280
  76.8 11.5 %collective-permute-start.13 = (bf16[4,256,128]{2,1,0:T(8,128)(2,1)}, bf16[4,256,128]{2,1,0:T(8,128)(2,1)}, u32[]{:S(2)}, u32[]{:S(2)}) collective-permute-start(bf16[4,256,128]{2,1,0:T(8,128)(2,1)} %add_tiles.18), channel_id=1, source_target_pairs={{0,2},{1,3},{2,0},{3,1},{4,6},{5,7},{6,4},{7,5},{8,10},{9,11},{10,... | collective-permute-start | bytes 786440 | tf_op jit(solution)/shard_map/ppermute | solution.py:280
  78.2 0.7 copy-start
  78.8 29.7 %collective-permute-start.17 = (bf16[4,256,128]{2,1,0:T(8,128)(2,1)S(1)}, bf16[4,256,128]{2,1,0:T(8,128)(2,1)}, u32[]{:S(2)}, u32[]{:S(2)}) collective-permute-start(bf16[4,256,128]{2,1,0:T(8,128)(2,1)S(1)} %add_tiles.20), channel_id=1, source_target_pairs={{0,6},{1,7},{2,4},{3,5},{4,2},{5,3},{6,0},{7,1},{8,14},{9,15},{10,... | collective-permute-start | bytes 786440 | tf_op jit(solution)/shard_map/ppermute | solution.py:280
  80.1 34.0 %collective-permute-start.19 = (bf16[4,256,128]{2,1,0:T(8,128)(2,1)S(1)}, bf16[4,256,128]{2,1,0:T(8,128)(2,1)}, u32[]{:S(2)}, u32[]{:S(2)}) collective-permute-start(bf16[4,256,128]{2,1,0:T(8,128)(2,1)S(1)} %add_tiles.21), channel_id=1, source_target_pairs={{0,7},{1,6},{2,5},{3,4},{4,3},{5,2},{6,1},{7,0},{8,15},{9,14},{10,... | collective-permute-start | bytes 786440 | tf_op jit(solution)/shard_map/ppermute | solution.py:280
  81.3 32.8 %collective-permute-start.21 = (bf16[4,256,128]{2,1,0:T(8,128)(2,1)S(1)}, bf16[4,256,128]{2,1,0:T(8,128)(2,1)}, u32[]{:S(2)}, u32[]{:S(2)}) collective-permute-start(bf16[4,256,128]{2,1,0:T(8,128)(2,1)S(1)} %add_tiles.22), channel_id=1, source_target_pairs={{0,1},{1,0},{2,3},{3,2},{4,5},{5,4},{6,7},{7,6},{8,9},{9,8},{10,11... | collective-permute-start | bytes 786440 | tf_op jit(solution)/shard_map/ppermute | solution.py:280
  84.9 23.7 %copy-start.1 = (bf16[2,256,128]{2,1,0:T(8,128)(2,1)S(1)}, bf16[2,256,128]{2,1,0:T(8,128)(2,1)}, u32[]{:S(2)}) copy-start(bf16[2,256,128]{2,1,0:T(8,128)(2,1)} %copy-done) | copy-start | bytes 393220
